TPU v7x, 128 devices: a whole 4x4x4 slice. The times are simulated.
128 devices in a mesh: depth: 4 (over z), col: 4 (over y), row: 8 (over x, core).
Axes of the slice: x: 4, y: 4, z: 4, core: 2. Of those that a mesh axis runs over, the one named last changes fastest.
Arguments:
- a_mat: bfloat16 [8192, 8192], P(('row', 'depth'), 'col')
- b_mat: bfloat16 [8192, 8192], P(('row', 'depth'), 'col')
Outputs:
- output: bfloat16 [8192, 8192], P(('row', 'depth'), 'col')
All inputs are finite; a program needn't handle non-finite values.
Results may differ from a plain program's by a relative error of at most 0.001.
Values are sent between devices in bfloat16 or wider.
A program may use at most 1 GiB of HBM per device.

v0:
```python
import jax
import jax.numpy as jnp
from jax import lax
from jax.sharding import PartitionSpec as P, NamedSharding


def solution(mesh):
    depth_n = mesh.shape["depth"]
    col_n = mesh.shape["col"]
    row_n = mesh.shape["row"]
    row_ratio = row_n // col_n
    layer_steps = row_n // depth_n
    all_axes = ("depth", "col", "row")

    def linear(layer, col_idx, row_idx):
        return (layer * col_n + col_idx) * row_n + row_idx

    def first_k(layer, row_idx):
        return (row_idx + layer * layer_steps) % row_n

    b_start = [
        (linear(layer, col_idx, (first_k(layer, row_idx) + col_idx * row_ratio) % row_n), linear(layer, col_idx, row_idx))
        for layer in range(depth_n) for col_idx in range(col_n) for row_idx in range(row_n)
    ]
    a_start = [
        (linear(layer, (col_idx + first_k(layer, row_idx) // row_ratio) % col_n, row_idx), linear(layer, col_idx, row_idx))
        for layer in range(depth_n) for col_idx in range(col_n) for row_idx in range(row_n)
    ]
    a_after = [
        (linear(layer, (col_idx + first_k(layer, row_idx) // row_ratio + 1) % col_n, row_idx), linear(layer, col_idx, row_idx))
        for layer in range(depth_n) for col_idx in range(col_n) for row_idx in range(row_n)
    ]
    b_shift = [((row_idx + 1) % row_n, row_idx) for row_idx in range(row_n)]
    a_shift = [((col_idx + 1) % col_n, col_idx) for col_idx in range(col_n)]

    def local_product(a_blk, b_blk):
        a_full = lax.all_gather(a_blk, "depth", axis=0, tiled=True)
        b_full = lax.all_gather(b_blk, "depth", axis=0, tiled=True)
        piece_w = a_full.shape[0]
        col_w = a_full.shape[1]
        b_cur = lax.ppermute(b_full, all_axes, b_start)
        a_lead = lax.ppermute(a_full, all_axes, a_start)
        if row_ratio == 1:
            queue = a_lead
        else:
            a_tail = lax.ppermute(a_full, all_axes, a_after)
            offset = (lax.axis_index("row") + lax.axis_index("depth") * layer_steps) % row_n % row_ratio
            joined = jnp.concatenate([a_lead, a_tail], axis=1)
            queue = lax.dynamic_slice_in_dim(joined, offset * piece_w, col_w, axis=1)
        pieces = [queue[:, slot * piece_w:(slot + 1) * piece_w] for slot in range(min(row_ratio, layer_steps))]
        part_sum = jnp.dot(pieces[0], b_cur, preferred_element_type=jnp.float32)
        for step in range(1, layer_steps):
            if step - 1 + row_ratio < layer_steps:
                pieces = pieces[1:] + [lax.ppermute(pieces[0], "col", a_shift)]
            else:
                pieces = pieces[1:]
            b_cur = lax.ppermute(b_cur, "row", b_shift)
            part_sum = part_sum + jnp.dot(pieces[0], b_cur, preferred_element_type=jnp.float32)
        c_part = lax.psum_scatter(part_sum, "depth", scatter_dimension=0, tiled=True)
        return c_part.astype(jnp.bfloat16)

    block_spec = P(("row", "depth"), "col")
    return jax.shard_map(local_product, mesh=mesh, in_specs=(block_spec, block_spec), out_specs=block_spec, check_vma=False)
```

profile of v0, /device:TPU:1, one launch (start us, length us, event | category | flops | bytes accessed | tf_op | source)
XLA Modules:
  0.0 404.4 jit_solution(14132051015657553308)
XLA Ops:
  6.5 0.0 all-gather.5.cloned.1.call-start
  6.5 0.7 all-gather.5.cloned.1.call-update
  7.3 0.0 all-gather.3.cloned.1.call-start
  7.3 0.7 all-gather.3.cloned.1.call-update
  8.0 0.0 reduce-scatter.2.cloned.1.call-start
  8.1 52.2 %all-gather.5.cloned.1.call-done = bf16[1024,2048]{1,0:T(8,128)(2,1)} async-done(((bf16[256,2048]{1,0:T(8,128)(2,1)}), bf16[1024,2048]{1,0:T(8,128)(2,1)}) %all-gather.5.cloned.1.call-update) | async-done | bytes 4194320 | tf_op jit(solution)/shard_map/all_gather | solution.py:38
  60.2 33.0 %collective-permute-start.2 = (bf16[1024,2048]{1,0:T(8,128)(2,1)}, bf16[1024,2048]{1,0:T(8,128)(2,1)}, u32[]{:S(2)}, u32[]{:S(2)}) collective-permute-start(bf16[1024,2048]{1,0:T(8,128)(2,1)} %all-gather.5.cloned.1.call-done), channel_id=1, source_target_pairs={{0,0},{1,1},{2,2},{3,3},{4,4},{5,5},{6,6},{7,7},{10,8},{11,9},{12,... | collective-permute-start | bytes 12582920 | tf_op jit(solution)/shard_map/ppermute | solution.py:41
  93.3 17.2 %all-gather.3.cloned.1.call-done = bf16[1024,2048]{1,0:T(8,128)(2,1)} async-done(((bf16[256,2048]{1,0:T(8,128)(2,1)}), bf16[1024,2048]{1,0:T(8,128)(2,1)}) %all-gather.3.cloned.1.call-update) | async-done | bytes 4194320 | tf_op jit(solution)/shard_map/all_gather | solution.py:37
  110.5 33.1 %collective-permute-start = (bf16[1024,2048]{1,0:T(8,128)(2,1)}, bf16[1024,2048]{1,0:T(8,128)(2,1)}, u32[]{:S(2)}, u32[]{:S(2)}) collective-permute-start(bf16[1024,2048]{1,0:T(8,128)(2,1)} %all-gather.3.cloned.1.call-done), channel_id=1, source_target_pairs={{0,0},{1,1},{10,2},{11,3},{20,4},{21,5},{30,6},{31,7},{8,8},{9,9},... | collective-permute-start | bytes 12582920 | tf_op jit(solution)/shard_map/ppermute | solution.py:42
  143.5 4.4 %collective-permute-start.1 = (bf16[1024,2048]{1,0:T(8,128)(2,1)}, bf16[1024,2048]{1,0:T(8,128)(2,1)}, u32[]{:S(2)}, u32[]{:S(2)}) collective-permute-start(bf16[1024,2048]{1,0:T(8,128)(2,1)} %all-gather.3.cloned.1.call-done), channel_id=1, source_target_pairs={{8,0},{9,1},{18,2},{19,3},{28,4},{29,5},{6,6},{7,7},{16,8},{17,9},... | collective-permute-start | bytes 12582920 | tf_op jit(solution)/shard_map/ppermute | solution.py:46
  147.9 0.0 collective-permute-done.2
  147.9 1.2 collective-permute-start.3
  149.1 0.0 collective-permute-done
  149.1 87.7 %collective-permute-done.1 = bf16[1024,2048]{1,0:T(8,128)(2,1)} collective-permute-done((bf16[1024,2048]{1,0:T(8,128)(2,1)}, bf16[1024,2048]{1,0:T(8,128)(2,1)}, u32[]{:S(2)}, u32[]{:S(2)}) %collective-permute-start.1) | collective-permute-done | bytes 4194336 | tf_op jit(solution)/shard_map/ppermute | solution.py:46
  236.9 3.6 fusion
  240.5 6.3 %fusion.2 = f32[1024,2048]{1,0:T(8,128)S(1)} fusion(bf16[1024,2048]{1,0:T(8,128)(2,1)} %collective-permute-done.2, bf16[1024,2048]{1,0:T(8,128)(2,1)S(1)} %fusion), kind=kOutput, calls=%fused_computation.5 | convolution fusion | flops 4294967296 | bytes 14680064 | tf_op jit(solution)/shard_map/dot_general | solution.py:51
  246.8 0.0 collective-permute-done.3
  246.8 9.0 %convolution_add_fusion = f32[1024,2048]{1,0:T(8,128)} fusion(f32[1024,2048]{1,0:T(8,128)S(1)} %fusion.2, bf16[1024,2048]{1,0:T(8,128)(2,1)} %collective-permute-done.3, bf16[1024,2048]{1,0:T(8,128)(2,1)S(1)} %fusion), kind=kOutput, calls=%fused_computation.3 | convolution fusion | flops 4297064448 | bytes 23068672 | tf_op jit(solution)/shard_map/dot_general | solution.py:58
  255.9 0.0 reduce-scatter.2.cloned.1.call-update
  255.9 139.3 %reduce-scatter.2.cloned.1.call-done = f32[256,2048]{1,0:T(8,128)} async-done(((f32[1024,2048]{1,0:T(8,128)}), f32[256,2048]{1,0:T(8,128)}) %reduce-scatter.2.cloned.1.call-update) | async-done | bytes 2097168 | tf_op jit(solution)/shard_map/reduce_scatter | solution.py:59
  395.2 2.7 convert_element_type.3
Async XLA Ops:
  6.5 53.7 %all-gather.5.cloned.1.call-start = ((), (), s32[]{:S(2)}) async-start(), calls=%async_computation.2 | async-start | bytes 5242880 | tf_op jit(solution)/shard_map/all_gather | solution.py:38
  7.3 103.2 %all-gather.3.cloned.1.call-start = ((), (), s32[]{:S(2)}) async-start(), calls=%async_computation.1 | async-start | bytes 5242880 | tf_op jit(solution)/shard_map/all_gather | solution.py:37
  8.0 387.2 %reduce-scatter.2.cloned.1.call-start = ((), (), s32[]{:S(2)}) async-start(), calls=%async_computation.3 | async-start | bytes 10485760 | tf_op jit(solution)/shard_map/reduce_scatter | solution.py:59
  60.2 87.7 %collective-permute-start.2 = (bf16[1024,2048]{1,0:T(8,128)(2,1)}, bf16[1024,2048]{1,0:T(8,128)(2,1)}, u32[]{:S(2)}, u32[]{:S(2)}) collective-permute-start(bf16[1024,2048]{1,0:T(8,128)(2,1)} %all-gather.5.cloned.1.call-done), channel_id=1, source_target_pairs={{0,0},{1,1},{2,2},{3,3},{4,4},{5,5},{6,6},{7,7},{10,8},{11,9},{12,... | collective-permute-start | bytes 12582920 | tf_op jit(solution)/shard_map/ppermute | solution.py:41
  110.5 38.7 %collective-permute-start = (bf16[1024,2048]{1,0:T(8,128)(2,1)}, bf16[1024,2048]{1,0:T(8,128)(2,1)}, u32[]{:S(2)}, u32[]{:S(2)}) collective-permute-start(bf16[1024,2048]{1,0:T(8,128)(2,1)} %all-gather.3.cloned.1.call-done), channel_id=1, source_target_pairs={{0,0},{1,1},{10,2},{11,3},{20,4},{21,5},{30,6},{31,7},{8,8},{9,9},... | collective-permute-start | bytes 12582920 | tf_op jit(solution)/shard_map/ppermute | solution.py:42
  143.5 93.3 %collective-permute-start.1 = (bf16[1024,2048]{1,0:T(8,128)(2,1)}, bf16[1024,2048]{1,0:T(8,128)(2,1)}, u32[]{:S(2)}, u32[]{:S(2)}) collective-permute-start(bf16[1024,2048]{1,0:T(8,128)(2,1)} %all-gather.3.cloned.1.call-done), channel_id=1, source_target_pairs={{8,0},{9,1},{18,2},{19,3},{28,4},{29,5},{6,6},{7,7},{16,8},{17,9},... | collective-permute-start | bytes 12582920 | tf_op jit(solution)/shard_map/ppermute | solution.py:46
  147.9 98.9 %collective-permute-start.3 = (bf16[1024,2048]{1,0:T(8,128)(2,1)}, bf16[1024,2048]{1,0:T(8,128)(2,1)}, u32[]{:S(2)}, u32[]{:S(2)}) collective-permute-start(bf16[1024,2048]{1,0:T(8,128)(2,1)} %collective-permute-done.2), channel_id=1, source_target_pairs={{1,0},{2,1},{3,2},{4,3},{5,4},{6,5},{7,6},{0,7},{9,8},{10,9},{11,1... | collective-permute-start | bytes 12582920 | tf_op jit(solution)/shard_map/ppermute | solution.py:57
Sparse Core Ops, SparseCore 0:
  9.0 51.1 all-gather.4
  61.9 48.5 all-gather.2
  256.0 139.1 reduce-scatter.1
where the time goes:
time: 409 us; the launch traced here: 404 us
  waiting for transfers between devices  298 us (73%)
  starting transfers between devices  71.8 us (18%)
  matrix products  15.3 us (4%)
  between operations  13.1 us (3%)
  other arithmetic  6.33 us (2%)
    reduce_scatter x1, waiting for transfers between devices, local_product(): lax.psum_scatter(part_sum, 'depth', scatter_dimension=0, tiled=True)  139 us
    ppermute x1, waiting for transfers between devices, local_product(): a_tail = lax.ppermute(a_full, all_axes, a_after)  87.7 us
    all_gather x1, waiting for transfers between devices, local_product(): b_full = lax.all_gather(b_blk, 'depth', axis=0, tiled=True)  52.2 us
    ppermute x1, starting transfers between devices, local_product(): a_lead = lax.ppermute(a_full, all_axes, a_start)  33.1 us
    ppermute x1, starting transfers between devices, local_product(): b_cur = lax.ppermute(b_full, all_axes, b_start)  33 us
    all_gather x1, waiting for transfers between devices, local_product(): a_full = lax.all_gather(a_blk, 'depth', axis=0, tiled=True)  17.2 us
    dot_general x1, matrix products, local_product(): jnp.dot(pieces[0], b_cur, preferred_element_type=jnp.float32)  9.03 us
  transfers between devices with their start and end apart: 7, of which 4 were waited for; matrix products, arithmetic and copies ran while one was open for 2% of the time, Pallas kernels for 0%

commit v1 on v0

v1 whole, which is shorter than its diff:
```python
import functools

import jax
import jax.numpy as jnp
from jax import lax
from jax.experimental import pallas as pl
from jax.experimental.pallas import tpu as pltpu
from jax.sharding import PartitionSpec as P

MESH = pl.DeviceIdType.MESH
GROUPS = 4


def kernel(a_ref, b_ref, out_ref, a_buf, b_buf, acc, stage, load_sem, y_recv, y_fwd, pair_recv, x_recv, x_fwd, z_recv, sib_recv, c_recv, send_sem):
    z, y, r = lax.axis_index("depth"), lax.axis_index("col"), lax.axis_index("row")
    x, c = r // 2, r % 2
    rows, width = a_ref.shape
    half = width // 2

    pair = z + 1 - 2 * (z % 2)
    mirror = 3 - z
    side = ((z + 1) // 2) % 2
    z_of = (z, mirror, pair, 3 - pair)

    y_peer = ({"col": (y + 1) % 4}, {"col": (y + 3) % 4})
    x_peer = ({"row": ((x + 1) % 4) * 2 + c}, {"row": ((x + 3) % 4) * 2 + c})
    to_pair, to_mirror, to_sibling = {"depth": pair}, {"depth": mirror}, {"row": x * 2 + 1 - c}
    peers = y_peer + x_peer + (to_pair, to_mirror, to_sibling)

    def remote(src, dst, kind, recv, where):
        return pltpu.make_async_remote_copy(src_ref=src, dst_ref=dst, send_sem=send_sem.at[kind], recv_sem=recv, device_id=where, device_id_type=MESH)

    def arrived(ref, recv):
        remote(ref, ref, 0, recv, to_sibling).wait_recv()

    def sent(ref, kind):
        remote(ref, ref, kind, z_recv.at[0], to_sibling).wait_send()

    own_rows, pair_rows = pl.ds(0, rows), pl.ds(rows, rows)
    part_rows = (own_rows, pair_rows)

    def a_load(g, cc):
        which = c + cc - 2 * c * cc
        start = pl.multiple_of(which * half + z_of[g] * rows, rows)
        return pltpu.make_async_copy(a_ref.at[:, pl.ds(start, rows)], a_buf.at[0, g, cc, own_rows], load_sem.at[g * 2 + cc])

    my_cols = pl.ds(pl.multiple_of(side * half, half), half)
    other_cols = pl.ds(pl.multiple_of((1 - side) * half, half), half)
    b_load = pltpu.make_async_copy(b_ref.at[:, my_cols], b_buf.at[0, 0, 0], load_sem.at[8])

    b_load.start()
    for g in (0, 2, 3, 1):
        for cc in range(2):
            a_load(g, cc).start()

    barrier = pltpu.get_barrier_semaphore()
    for where in peers:
        pl.semaphore_signal(barrier, inc=1, device_id=where, device_id_type=MESH)
    pl.semaphore_wait(barrier, len(peers))

    slot_of = (3, 1)
    k_half = (pl.ds(0, rows // 2), pl.ds(rows // 2, rows // 2))

    def send_x(g):
        for d in range(2):
            for h in (d, 1 - d):
                remote(b_buf.at[0, g, 0, k_half[h]], b_buf.at[slot_of[d], g, 0, k_half[h]], 0, x_recv.at[d, g, h], x_peer[d]).start()

    def forward_x(g, d):
        arrived(b_buf.at[slot_of[d], g, 0, k_half[d]], x_recv.at[d, g, d])
        remote(b_buf.at[slot_of[d], g, 0, k_half[d]], b_buf.at[2, g, 0, k_half[d]], 0, x_fwd.at[d, g], x_peer[d]).start()

    def send_y(g, part):
        for d in range(2):
            for cc in (d, 1 - d):
                remote(a_buf.at[0, g, cc, part_rows[part]], a_buf.at[slot_of[d], g, cc, part_rows[part]], 1, y_recv.at[d, g, part, cc], y_peer[d]).start()

    def forward_y(g, part, d):
        arrived(a_buf.at[slot_of[d], g, d, part_rows[part]], y_recv.at[d, g, part, d])
        remote(a_buf.at[slot_of[d], g, d, part_rows[part]], a_buf.at[2, g, d, part_rows[part]], 1, y_fwd.at[d, g, part], y_peer[d]).start()

    def send_pair(g):
        for cc in range(2):
            remote(a_buf.at[0, (g + 2) % 4, cc, own_rows], a_buf.at[0, g, cc, pair_rows], 2, pair_recv.at[g, cc], to_pair).start()

    def pair_arrived(g):
        for cc in range(2):
            arrived(a_buf.at[0, g, cc, pair_rows], pair_recv.at[g, cc])

    def send_sibling(j, g):
        remote(b_buf.at[j, g, 0], b_buf.at[j, g, 1], 4, sib_recv.at[j, g], to_sibling).start()

    b_load.wait()
    send_x(0)
    remote(b_buf.at[0, 0, 0], b_buf.at[0, 1, 0], 3, z_recv.at[1], to_mirror).start()
    for cc in range(2):
        a_load(0, cc).wait()
    send_y(0, 0)
    for cc in range(2):
        a_load(2, cc).wait()
    send_pair(0)
    for cc in range(2):
        a_load(3, cc).wait()
    send_pair(1)
    remote(b_ref.at[:, other_cols], b_buf.at[0, 2, 0], 3, z_recv.at[2], to_pair).start()
    send_pair(2)
    for cc in range(2):
        a_load(1, cc).wait()
    send_pair(3)
    send_sibling(0, 0)
    pair_arrived(0)
    send_y(0, 1)

    tile = half // 4

    def compute(g):
        slots = [(x + j - y + 4) % 4 for j in range(4)]

        def product(part, n):
            cols = pl.ds(pl.multiple_of(n * tile, tile), tile)
            total = None
            for j in range(4):
                for cc in range(2):
                    term = jnp.dot(a_buf[slots[j], g, cc, part_rows[part], :], b_buf[j, g, cc, :, cols], preferred_element_type=jnp.float32)
                    total = term if total is None else total + term
            return cols, total

        for part in (1, 0):
            def body(n, carry, part=part):
                cols, total = product(part, n)
                if g == 0:
                    acc[part_rows[part], cols] = total
                elif g < GROUPS - 1:
                    acc[part_rows[part], cols] += total
                else:
                    stage[part, :, cols] = (acc[part_rows[part], cols] + total).astype(stage.dtype)
                return carry

            lax.fori_loop(0, 4, body, 0)
            if g == GROUPS - 1 and part == 1:
                remote(stage.at[1], out_ref.at[:, my_cols], 5, c_recv, to_pair).start()

    def finish_group(g):
        for part in range(2):
            for d in range(2):
                arrived(a_buf.at[slot_of[d], g, 1 - d, part_rows[part]], y_recv.at[d, g, part, 1 - d])
                arrived(a_buf.at[2, g, d, part_rows[part]], y_fwd.at[d, g, part])
        for j in range(4):
            arrived(b_buf.at[j, g, 1], sib_recv.at[j, g])

    def opposite_arrived(g):
        for d in range(2):
            arrived(b_buf.at[2, g, 0, k_half[d]], x_fwd.at[d, g])
        send_sibling(2, g)

    for g in range(GROUPS):
        for d in range(2):
            forward_y(g, 0, d)
        if g > 0:
            opposite_arrived(g - 1)
        for d in range(2):
            forward_x(g, d)
        for d in range(2):
            forward_y(g, 1, d)
        if g + 1 < GROUPS:
            arrived(b_buf.at[0, g + 1, 0], z_recv.at[g + 1])
            send_x(g + 1)
            send_y(g + 1, 0)
            pair_arrived(g + 1)
            send_y(g + 1, 1)
            if g + 1 == 2:
                remote(b_buf.at[0, 2, 0], b_buf.at[0, 3, 0], 3, z_recv.at[3], to_mirror).start()
            send_sibling(0, g + 1)
        for d in range(2):
            arrived(b_buf.at[slot_of[d], g, 0, k_half[1 - d]], x_recv.at[d, g, 1 - d])
            send_sibling(slot_of[d], g)
        if g > 0:
            finish_group(g - 1)
            compute(g - 1)

    opposite_arrived(GROUPS - 1)
    finish_group(GROUPS - 1)
    compute(GROUPS - 1)
    own_out = pltpu.make_async_copy(stage.at[0], out_ref.at[:, my_cols], load_sem.at[9])
    own_out.start()

    sent(b_buf.at[pl.ds(0, 3), :, 0], 0)
    sent(a_buf.at[pl.ds(0, 3)], 1)
    sent(a_buf.at[0, :, :, own_rows], 2)
    sent(b_buf.at[0, pl.ds(0, 3), 0], 3)
    sent(b_buf.at[:, :, 0], 4)
    sent(stage.at[1], 5)
    arrived(out_ref.at[:, other_cols], c_recv)
    own_out.wait()


def solution(mesh):
    def product(a_blk, b_blk):
        rows, width = a_blk.shape
        half = width // 2
        dma = pltpu.SemaphoreType.DMA
        return pl.pallas_call(
            kernel,
            out_shape=jax.ShapeDtypeStruct((rows, width), jnp.bfloat16),
            in_specs=[pl.BlockSpec(memory_space=pl.ANY)] * 2,
            out_specs=pl.BlockSpec(memory_space=pl.ANY),
            scratch_shapes=[
                pltpu.VMEM((4, GROUPS, 2, 2 * rows, rows), jnp.bfloat16),
                pltpu.VMEM((4, GROUPS, 2, rows, half), jnp.bfloat16),
                pltpu.VMEM((2 * rows, half), jnp.float32),
                pltpu.VMEM((2, rows, half), jnp.bfloat16),
                dma((10,)),
                dma((2, GROUPS, 2, 2)),
                dma((2, GROUPS, 2)),
                dma((GROUPS, 2)),
                dma((2, GROUPS, 2)),
                dma((2, GROUPS)),
                dma((GROUPS,)),
                dma((4, GROUPS)),
                dma(()),
                dma((6,)),
            ],
            compiler_params=pltpu.CompilerParams(collective_id=0, has_side_effects=True, vmem_limit_bytes=48 * 1024 * 1024),
        )(a_blk, b_blk)

    block_spec = P(("row", "depth"), "col")
    return jax.shard_map(product, mesh=mesh, in_specs=(block_spec, block_spec), out_specs=block_spec, check_vma=False)
```

time: 409 us -> 97.3 us (0.24); the launches traced: 404 us -> 97.1 us
  waiting for transfers between devices: 298 us -> 0 us
  Pallas kernels: 0 us -> 93.7 us
  starting transfers between devices: 71.8 us -> 0 us
  matrix products: 15.3 us -> 0 us
  between operations: 13.1 us -> 0.01 us
  other arithmetic: 6.33 us -> 0 us
    reduce_scatter x1 -> x0, waiting for transfers between devices: 139 us -> none  [local_product(): lax.psum_scatter(part_sum, 'depth', scatter_dimension=0, tiled=True)]
    pallas_call x0 -> x1, Pallas kernels: none -> 93.7 us  [product(): pl.pallas_call(kernel, out_shape=jax.ShapeDtypeStruct((rows, width), jnp....]
    ppermute x4 -> x0, waiting for transfers between devices: 87.7 us -> none  [the longest x1 87.7 us: local_product(): a_tail = lax.ppermute(a_full, all_axes, a_after)]
    ppermute x4 -> x0, starting transfers between devices: 71.7 us -> none  [the longest x1 33.1 us: local_product(): a_lead = lax.ppermute(a_full, all_axes, a_start)]
    all_gather x2 -> x0, waiting for transfers between devices: 69.4 us -> none  [the longest x1 52.2 us: local_product(): b_full = lax.all_gather(b_blk, 'depth', axis=0, tiled=True)]
    dot_general x2 -> x0, matrix products: 15.3 us -> none  [the longest x1 9.03 us: local_product(): jnp.dot(pieces[0], b_cur, preferred_element_type=jnp.float32)]
  transfers between devices with their start and end apart: 7 -> 0, of which waited for: 4 -> 0; matrix products, arithmetic and copies ran while one was open for 2% -> 0% of each run, Pallas kernels for 0% -> 0%
where the time goes in v1:
time: 97.3 us; the launch traced here: 97.1 us
  Pallas kernels  93.7 us (96%)
  local copies, waits for them, and re-layouts  3.42 us (4%)
    pallas_call x1, Pallas kernels, product(): pl.pallas_call(kernel, out_shape=jax.ShapeDtypeStruct((rows, width), jnp....  93.7 us
    unnamed x5, local copies, waits for them, and re-layouts  3.42 us

profile of v1, /device:TPU:1, one launch (start us, length us, event | category | flops | bytes accessed | tf_op | source)
XLA Modules:
  0.0 97.1 jit_solution(17561043487852788283)
XLA Ops:
  0.0 0.0 copy-start
  0.0 1.2 %copy-done = bf16[256,2048]{1,0:T(8,128)(2,1)S(1)} copy-done((bf16[256,2048]{1,0:T(8,128)(2,1)S(1)}, bf16[256,2048]{1,0:T(8,128)(2,1)}, u32[]{:S(2)}) %copy-start) | copy-done | bytes 1048600
  1.2 0.0 copy-start.1
  1.2 1.2 %copy-done.1 = bf16[256,2048]{1,0:T(8,128)(2,1)S(1)} copy-done((bf16[256,2048]{1,0:T(8,128)(2,1)S(1)}, bf16[256,2048]{1,0:T(8,128)(2,1)}, u32[]{:S(2)}) %copy-start.1) | copy-done | bytes 1048600
  2.5 93.7 %shard_map.28 = bf16[256,2048]{1,0:T(8,128)(2,1)S(1)} custom-call(bf16[256,2048]{1,0:T(8,128)(2,1)S(1)} %copy-done, bf16[256,2048]{1,0:T(8,128)(2,1)S(1)} %copy-done.1), custom_call_target="tpu_custom_call" | custom-call | tf_op jit(solution)/shard_map/pallas_call | solution.py:202
  96.1 1.0 %copy.4 = bf16[256,2048]{1,0:T(8,128)(2,1)} copy(bf16[256,2048]{1,0:T(8,128)(2,1)S(1)} %shard_map.28) | data formatting | bytes 2097152
Async XLA Ops:
  0.0 1.2 %copy-start = (bf16[256,2048]{1,0:T(8,128)(2,1)S(1)}, bf16[256,2048]{1,0:T(8,128)(2,1)}, u32[]{:S(2)}) copy-start(bf16[256,2048]{1,0:T(8,128)(2,1)} %a_ref.1) | copy-start | bytes 3145732
  1.2 1.2 %copy-start.1 = (bf16[256,2048]{1,0:T(8,128)(2,1)S(1)}, bf16[256,2048]{1,0:T(8,128)(2,1)}, u32[]{:S(2)}) copy-start(bf16[256,2048]{1,0:T(8,128)(2,1)} %b_ref.1) | copy-start | bytes 3145732

commit v2 on v1

v2 whole, which is shorter than its diff:
```python
import jax
import jax.numpy as jnp
from jax import lax
from jax.experimental import pallas as pl
from jax.experimental.pallas import tpu as pltpu
from jax.sharding import PartitionSpec as P

MESH = pl.DeviceIdType.MESH
GROUPS = 4
X_STEPS = ((0, 0, 2), (1, 0, 2), (2, 0, 2), (3, 0, 1), (3, 1, 1))
X_KIND, Y_KIND, PAIR_A, Z_KIND, SIBLING, C_KIND, Z_LATE, SIBLING_LATE, X_MINE, X_OTHER = range(10)


def kernel(a_ref, b_ref, out_ref, a_buf, b_buf, other_buf, acc, stage, load_sem, y_recv, y_fwd, pair_recv, x_recv, x_fwd, late_recv, late_fwd, z_recv, z_late, sib_recv, sib_late, c_recv, send_sem):
    z, y, r = lax.axis_index("depth"), lax.axis_index("col"), lax.axis_index("row")
    x, c = r // 2, r % 2
    rows, width = a_ref.shape
    half = width // 2
    late = rows // 4
    early = rows - late

    pair = z + 1 - 2 * (z % 2)
    mirror = 3 - z
    side = ((z + 1) // 2) % 2
    z_of = (z, mirror, pair, 3 - pair)

    y_peer = ({"col": (y + 1) % 4}, {"col": (y + 3) % 4})
    x_peer = ({"row": ((x + 1) % 4) * 2 + c}, {"row": ((x + 3) % 4) * 2 + c})
    to_pair, to_mirror, to_sibling = {"depth": pair}, {"depth": mirror}, {"row": x * 2 + 1 - c}
    peers = y_peer + x_peer + (to_pair, to_mirror, to_sibling)

    def remote(src, dst, kind, recv, where):
        return pltpu.make_async_remote_copy(src_ref=src, dst_ref=dst, send_sem=send_sem.at[kind], recv_sem=recv, device_id=where, device_id_type=MESH)

    def arrived(ref, recv):
        remote(ref, ref, 0, recv, to_sibling).wait_recv()

    def sent(ref, kind):
        remote(ref, ref, kind, z_recv.at[0], to_sibling).wait_send()

    part_rows = (pl.ds(0, rows), pl.ds(rows, rows))
    early_rows, late_rows = pl.ds(0, early), pl.ds(early, late)
    early_half = (pl.ds(0, early // 2), pl.ds(early // 2, early // 2))
    late_half = (pl.ds(early, late // 2), pl.ds(early + late // 2, late // 2))
    other_half = (pl.ds(0, late // 2), pl.ds(late // 2, late // 2))
    my_cols = pl.ds(pl.multiple_of(side * half, half), half)
    other_cols = pl.ds(pl.multiple_of((1 - side) * half, half), half)

    def step_cols(s):
        _, first, count = X_STEPS[s]
        return pl.ds(first * (half // 2), count * (half // 2))

    def a_load(g, cc):
        which = c + cc - 2 * c * cc
        start = pl.multiple_of(which * half + z_of[g] * rows, rows)
        return pltpu.make_async_copy(a_ref.at[:, pl.ds(start, rows)], a_buf.at[0, g, cc, part_rows[0]], load_sem.at[g * 2 + cc])

    def a_loaded(g):
        for cc in range(2):
            a_load(g, cc).wait()

    b_load = pltpu.make_async_copy(b_ref.at[:, my_cols], b_buf.at[0, 0, 0], load_sem.at[8])
    other_load = pltpu.make_async_copy(b_ref.at[late_rows, other_cols], other_buf.at[0], load_sem.at[9])
    b_load.start()
    other_load.start()
    for g in (0, 2, 3, 1):
        for cc in range(2):
            a_load(g, cc).start()

    barrier = pltpu.get_barrier_semaphore()
    for where in peers:
        pl.semaphore_signal(barrier, inc=1, device_id=where, device_id_type=MESH)
    pl.semaphore_wait(barrier, len(peers))

    slot_of = (3, 1)

    def send_x(s):
        g, cols = X_STEPS[s][0], step_cols(s)
        for d in range(2):
            for h in (d, 1 - d):
                remote(b_buf.at[0, g, 0, early_half[h], cols], b_buf.at[slot_of[d], g, 0, early_half[h], cols], X_KIND, x_recv.at[d, s, h], x_peer[d]).start()

    def forward_x(s):
        g, cols = X_STEPS[s][0], step_cols(s)
        for d in range(2):
            got = b_buf.at[slot_of[d], g, 0, early_half[d], cols]
            arrived(got, x_recv.at[d, s, d])
            remote(got, b_buf.at[2, g, 0, early_half[d], cols], X_KIND, x_fwd.at[d, s], x_peer[d]).start()

    def send_sibling(j, s):
        g, cols = X_STEPS[s][0], step_cols(s)
        remote(b_buf.at[j, g, 0, early_rows, cols], b_buf.at[j, g, 1, early_rows, cols], SIBLING, sib_recv.at[j, s], to_sibling).start()

    def sibling_arrived(s):
        g, cols = X_STEPS[s][0], step_cols(s)
        for j in range(4):
            arrived(b_buf.at[j, g, 1, early_rows, cols], sib_recv.at[j, s])

    def finish_x(s):
        g, cols = X_STEPS[s][0], step_cols(s)
        for d in range(2):
            arrived(b_buf.at[slot_of[d], g, 0, early_half[1 - d], cols], x_recv.at[d, s, 1 - d])
            send_sibling(slot_of[d], s)
        for d in range(2):
            arrived(b_buf.at[2, g, 0, early_half[d], cols], x_fwd.at[d, s])
        send_sibling(2, s)

    def send_sibling_late(g):
        remote(b_buf.at[:, g, 0, late_rows], b_buf.at[:, g, 1, late_rows], SIBLING_LATE, sib_late.at[g], to_sibling).start()

    def sibling_late_arrived(g):
        arrived(b_buf.at[:, g, 1, late_rows], sib_late.at[g])

    def late_refs(slot, h):
        return b_buf.at[slot, 0, 0, late_half[h]], other_buf.at[slot, other_half[h]]

    def send_late_x():
        for k in range(2):
            for d in range(2):
                for h in (d, 1 - d):
                    remote(late_refs(0, h)[k], late_refs(slot_of[d], h)[k], X_MINE + k, late_recv.at[d, k, h], x_peer[d]).start()

    def forward_late_x(k):
        for d in range(2):
            got = late_refs(slot_of[d], d)[k]
            arrived(got, late_recv.at[d, k, d])
            remote(got, late_refs(2, d)[k], X_MINE + k, late_fwd.at[d, k], x_peer[d]).start()

    def late_x_arrived(k):
        for d in range(2):
            arrived(late_refs(slot_of[d], 1 - d)[k], late_recv.at[d, k, 1 - d])
            arrived(late_refs(2, d)[k], late_fwd.at[d, k])

    def late_slots(g, u):
        return b_buf.at[pl.ds(2 * u, 2), g, 0, late_rows]

    def send_z_late(src, g, u, where):
        remote(src, late_slots(g, u), Z_LATE, z_late.at[g, u], where).start()

    def send_y(g, part):
        for d in range(2):
            for cc in (d, 1 - d):
                remote(a_buf.at[0, g, cc, part_rows[part]], a_buf.at[slot_of[d], g, cc, part_rows[part]], Y_KIND, y_recv.at[d, g, part, cc], y_peer[d]).start()

    def forward_y(g, part):
        for d in range(2):
            got = a_buf.at[slot_of[d], g, d, part_rows[part]]
            arrived(got, y_recv.at[d, g, part, d])
            remote(got, a_buf.at[2, g, d, part_rows[part]], Y_KIND, y_fwd.at[d, g, part], y_peer[d]).start()

    def near_y_arrived(g, part):
        for d in range(2):
            arrived(a_buf.at[slot_of[d], g, 1 - d, part_rows[part]], y_recv.at[d, g, part, 1 - d])

    def far_y_arrived(g, part):
        for d in range(2):
            arrived(a_buf.at[2, g, d, part_rows[part]], y_fwd.at[d, g, part])

    def finish_y(g, part):
        near_y_arrived(g, part)
        far_y_arrived(g, part)

    def send_pair(g):
        for cc in range(2):
            remote(a_buf.at[0, (g + 2) % 4, cc, part_rows[0]], a_buf.at[0, g, cc, part_rows[1]], PAIR_A, pair_recv.at[g, cc], to_pair).start()

    def pair_arrived(g):
        for cc in range(2):
            arrived(a_buf.at[0, g, cc, part_rows[1]], pair_recv.at[g, cc])

    tile = half // 4

    def compute(g, part, first, count, slots=(0, 1, 2, 3), last=False):
        def body(n, carry):
            cols = pl.ds(pl.multiple_of(n * tile, tile), tile)
            total = None
            for i in slots:
                j = (y + i - x + 4) % 4
                for cc in range(2):
                    term = jnp.dot(a_buf[i, g, cc, part_rows[part], :], b_buf[j, g, cc, :, cols], preferred_element_type=jnp.float32)
                    total = term if total is None else total + term
            if g > 0 or len(slots) < 4:
                total = total + acc[part_rows[part], cols]
            if last:
                stage[part, :, cols] = total.astype(stage.dtype)
            else:
                acc[part_rows[part], cols] = total
            return carry

        lax.fori_loop(first, first + count, body, 0)

    def out_cols(of_side, k):
        return pl.ds(pl.multiple_of(of_side * half + k * (half // 2), half // 2), half // 2)

    def send_c(k):
        remote(stage.at[1, :, pl.ds(k * (half // 2), half // 2)], out_ref.at[:, out_cols(side, k)], C_KIND, c_recv.at[k], to_pair).start()

    b_load.wait()
    other_load.wait()
    send_late_x()
    remote(b_buf.at[0, 0, 0, early_rows], b_buf.at[0, 1, 0, early_rows], Z_KIND, z_recv.at[1], to_mirror).start()
    a_loaded(0)
    send_y(0, 0)
    a_loaded(2)
    send_pair(0)
    send_x(0)
    a_loaded(3)
    send_pair(1)
    remote(b_ref.at[early_rows, other_cols], b_buf.at[0, 2, 0, early_rows], Z_KIND, z_recv.at[2], to_pair).start()
    send_pair(2)
    a_loaded(1)
    send_pair(3)
    send_sibling(0, 0)

    forward_late_x(0)
    forward_y(0, 0)
    forward_late_x(1)
    pair_arrived(0)
    send_y(0, 1)
    late_x_arrived(0)
    for u in range(2):
        send_z_late(late_slots(0, u), 1, u, to_mirror)
    send_sibling_late(0)
    late_x_arrived(1)
    for u in range(2):
        send_z_late(other_buf.at[pl.ds(2 * u, 2)], 2, u, to_pair)

    forward_y(0, 1)
    send_y(1, 0)
    pair_arrived(1)
    send_y(1, 1)
    forward_x(0)
    arrived(b_buf.at[0, 1, 0, early_rows], z_recv.at[1])
    send_x(1)
    send_sibling(0, 1)

    finish_x(0)
    arrived(b_buf.at[0, 2, 0, early_rows], z_recv.at[2])
    remote(b_buf.at[0, 2, 0, early_rows], b_buf.at[0, 3, 0, early_rows], Z_KIND, z_recv.at[3], to_mirror).start()
    send_sibling(0, 2)
    forward_y(1, 0)
    for u in range(2):
        arrived(late_slots(1, u), z_late.at[1, u])
    send_sibling_late(1)
    forward_x(1)
    send_x(2)
    forward_y(1, 1)
    pair_arrived(2)
    send_y(2, 1)
    pair_arrived(3)
    send_y(3, 1)

    for part in range(2):
        finish_y(0, part)
    sibling_arrived(0)
    sibling_late_arrived(0)
    compute(0, 1, 0, 4)
    compute(0, 0, 0, 4)

    finish_x(1)
    forward_y(2, 1)
    arrived(b_buf.at[0, 3, 0, early_rows], z_recv.at[3])
    forward_x(2)
    send_x(3)
    send_x(4)
    send_sibling(0, 3)
    send_sibling(0, 4)
    for u in range(2):
        arrived(late_slots(2, u), z_late.at[2, u])
        send_z_late(late_slots(2, u), 3, u, to_mirror)
    send_sibling_late(2)

    for part in range(2):
        finish_y(1, part)
    sibling_arrived(1)
    sibling_late_arrived(1)
    compute(1, 1, 0, 4)
    forward_y(3, 1)
    send_y(2, 0)
    send_y(3, 0)
    compute(1, 0, 0, 4)

    finish_x(2)
    forward_x(3)
    for u in range(2):
        arrived(late_slots(3, u), z_late.at[3, u])
    send_sibling_late(3)
    finish_y(2, 1)
    sibling_arrived(2)
    sibling_late_arrived(2)
    compute(2, 1, 0, 4)

    finish_x(3)
    forward_y(2, 0)
    forward_x(4)
    finish_y(3, 1)
    sibling_arrived(3)
    sibling_late_arrived(3)
    compute(3, 1, 0, 2, last=True)
    send_c(0)

    finish_x(4)
    sibling_arrived(4)
    compute(3, 1, 2, 2, last=True)
    send_c(1)
    forward_y(3, 0)
    finish_y(2, 0)
    compute(2, 0, 0, 4)
    near_y_arrived(3, 0)
    compute(3, 0, 0, 4, slots=(0, 1, 3))
    far_y_arrived(3, 0)
    own_out = []
    for k in range(2):
        compute(3, 0, 2 * k, 2, slots=(2,), last=True)
        own_out.append(pltpu.make_async_copy(stage.at[0, :, pl.ds(k * (half // 2), half // 2)], out_ref.at[:, out_cols(side, k)], load_sem.at[10 + k]))
        own_out[k].start()

    sent(b_buf.at[pl.ds(0, 3), :, 0, early_rows], X_KIND)
    sent(a_buf.at[pl.ds(0, 3)], Y_KIND)
    sent(a_buf.at[0, :, :, part_rows[0]], PAIR_A)
    sent(b_buf.at[0, pl.ds(0, 3), 0, early_rows], Z_KIND)
    sent(b_buf.at[:, :, 0, early_rows], SIBLING)
    sent(b_buf.at[:, pl.ds(0, 3), 0, late_rows], Z_LATE)
    sent(b_buf.at[:, :, 0, late_rows], SIBLING_LATE)
    sent(b_buf.at[pl.ds(0, 3), 0, 0, late_rows], X_MINE)
    sent(other_buf.at[pl.ds(0, 3)], X_OTHER)
    sent(stage.at[1], C_KIND)
    for k in range(2):
        arrived(out_ref.at[:, out_cols(1 - side, k)], c_recv.at[k])
    for copy in own_out:
        copy.wait()


def solution(mesh):
    def product(a_blk, b_blk):
        rows, width = a_blk.shape
        half = width // 2
        dma = pltpu.SemaphoreType.DMA
        return pl.pallas_call(
            kernel,
            out_shape=jax.ShapeDtypeStruct((rows, width), jnp.bfloat16),
            in_specs=[pl.BlockSpec(memory_space=pltpu.HBM)] * 2,
            out_specs=pl.BlockSpec(memory_space=pltpu.HBM),
            scratch_shapes=[
                pltpu.VMEM((4, GROUPS, 2, 2 * rows, rows), jnp.bfloat16),
                pltpu.VMEM((4, GROUPS, 2, rows, half), jnp.bfloat16),
                pltpu.VMEM((4, rows // 4, half), jnp.bfloat16),
                pltpu.VMEM((2 * rows, half), jnp.float32),
                pltpu.VMEM((2, rows, half), jnp.bfloat16),
                dma((12,)),
                dma((2, GROUPS, 2, 2)),
                dma((2, GROUPS, 2)),
                dma((GROUPS, 2)),
                dma((2, len(X_STEPS), 2)),
                dma((2, len(X_STEPS))),
                dma((2, 2, 2)),
                dma((2, 2)),
                dma((GROUPS,)),
                dma((GROUPS, 2)),
                dma((4, len(X_STEPS))),
                dma((GROUPS,)),
                dma((2,)),
                dma((10,)),
            ],
            compiler_params=pltpu.CompilerParams(collective_id=0, has_side_effects=True, vmem_limit_bytes=60 * 1024 * 1024),
        )(a_blk, b_blk)

    block_spec = P(("row", "depth"), "col")
    return jax.shard_map(product, mesh=mesh, in_specs=(block_spec, block_spec), out_specs=block_spec, check_vma=False)
```

time: 97.3 us -> 87.4 us (0.90); the launches traced: 97.1 us -> 86.2 us
  Pallas kernels: 93.7 us -> 83.8 us
  local copies, waits for them, and re-layouts: 3.42 us -> 2.3 us
    pallas_call x1, Pallas kernels: 93.7 us -> 83.8 us  [product(): pl.pallas_call(kernel, out_shape=jax.ShapeDtypeStruct((rows, width), jnp....]
    unnamed x5 -> x1, local copies, waits for them, and re-layouts: 3.42 us -> 2.3 us
where the time goes in v2:
time: 87.4 us; the launch traced here: 86.2 us
  Pallas kernels  83.8 us (96%)
  local copies, waits for them, and re-layouts  2.3 us (3%)
    pallas_call x1, Pallas kernels, product(): pl.pallas_call(kernel, out_shape=jax.ShapeDtypeStruct((rows, width), jnp....  83.8 us
    unnamed x1, local copies, waits for them, and re-layouts  2.3 us

profile of v2, /device:TPU:1, one launch (start us, length us, event | category | flops | bytes accessed | tf_op | source)
XLA Modules:
  0.0 86.2 jit_solution(13632489874356609165)
XLA Ops:
  0.0 83.8 %shard_map.28 = bf16[256,2048]{1,0:T(8,128)(2,1)} custom-call(bf16[256,2048]{1,0:T(8,128)(2,1)} %a_ref.1, bf16[256,2048]{1,0:T(8,128)(2,1)} %b_ref.1), custom_call_target="tpu_custom_call" | custom-call | tf_op jit(solution)/shard_map/pallas_call | solution.py:339
  83.8 2.3 %copy.4 = bf16[256,2048]{1,0:T(8,128)(2,1)} copy(bf16[256,2048]{1,0:T(8,128)(2,1)} %shard_map.28) | data formatting | bytes 2097152

commit v3 on v1

v3 whole, which is shorter than its diff:
```python
import jax
import jax.numpy as jnp
from jax import lax
from jax.experimental import pallas as pl
from jax.experimental.pallas import tpu as pltpu
from jax.sharding import PartitionSpec as P

MESH = pl.DeviceIdType.MESH
GROUPS = 4
X_STEPS = ((0, False, 0, 4), (1, True, 0, 4), (2, False, 0, 4), (3, False, 0, 2), (3, False, 2, 1), (3, False, 3, 1))
C_PIECES = ((0, 2), (2, 1), (3, 1))
X_KIND, X_EARLY, Y_OWN, Y_PAIR, PAIR_A, PAIR_FULL, Z_KIND, Z_EARLY, Z_LATE, SIBLING, C_KIND = range(11)


def kernel(a_ref, b_ref, out_ref, a_buf, b_buf, acc, stage, load_sem, y_recv, y_fwd, pair_recv, pair_full, x_recv, x_fwd, z_recv, z_late, sib_recv, sib_late, c_recv, send_sem):
    z, y, r = lax.axis_index("depth"), lax.axis_index("col"), lax.axis_index("row")
    x, c = r // 2, r % 2
    rows, width = a_ref.shape
    half = width // 2
    tile = half // 4
    early = rows // 4

    pair = z + 1 - 2 * (z % 2)
    mirror = 3 - z
    side = ((z + 1) // 2) % 2
    z_of = (z, mirror, pair, 3 - pair)

    y_peer = ({"col": (y + 1) % 4}, {"col": (y + 3) % 4})
    x_peer = ({"row": ((x + 1) % 4) * 2 + c}, {"row": ((x + 3) % 4) * 2 + c})
    to_pair, to_mirror, to_sibling = {"depth": pair}, {"depth": mirror}, {"row": x * 2 + 1 - c}
    peers = y_peer + x_peer + (to_pair, to_mirror, to_sibling)

    def remote(src, dst, kind, recv, where):
        return pltpu.make_async_remote_copy(src_ref=src, dst_ref=dst, send_sem=send_sem.at[kind], recv_sem=recv, device_id=where, device_id_type=MESH)

    def arrived(ref, recv):
        remote(ref, ref, 0, recv, to_sibling).wait_recv()

    def sent(ref, kind):
        remote(ref, ref, kind, z_recv.at[0], to_sibling).wait_send()

    part_rows = (pl.ds(0, rows), pl.ds(rows, rows))
    early_rows, late_rows = pl.ds(0, early), pl.ds(early, rows - early)
    my_cols = pl.ds(pl.multiple_of(side * half, half), half)
    other_cols = pl.ds(pl.multiple_of((1 - side) * half, half), half)

    def a_load(g, cc):
        which = c + cc - 2 * c * cc
        start = pl.multiple_of(which * half + z_of[g] * rows, rows)
        return pltpu.make_async_copy(a_ref.at[:, pl.ds(start, rows)], a_buf.at[0, g, cc, part_rows[0]], load_sem.at[g * 2 + cc])

    def a_loaded(g):
        for cc in range(2):
            a_load(g, cc).wait()

    b_load = pltpu.make_async_copy(b_ref.at[:, my_cols], b_buf.at[0, 0, 0], load_sem.at[8])
    b_load.start()
    for g in (0, 2, 3, 1):
        for cc in range(2):
            a_load(g, cc).start()

    barrier = pltpu.get_barrier_semaphore()
    for where in peers:
        pl.semaphore_signal(barrier, inc=1, device_id=where, device_id_type=MESH)
    pl.semaphore_wait(barrier, len(peers))

    slot_of = (3, 1)

    def step_refs(s, slot, piece=None, core=0):
        g, early_only, first, count = X_STEPS[s]
        size = early if early_only else rows
        at = pl.ds(0, size) if piece is None else pl.ds(piece * (size // 2), size // 2)
        return b_buf.at[slot, g, core, at, pl.ds(first * tile, count * tile)]

    def x_kind(s):
        return X_EARLY if X_STEPS[s][1] else X_KIND

    def send_x(s):
        for d in range(2):
            for h in (d, 1 - d):
                remote(step_refs(s, 0, h), step_refs(s, slot_of[d], h), x_kind(s), x_recv.at[d, s, h], x_peer[d]).start()

    def forward_x(s):
        for d in range(2):
            arrived(step_refs(s, slot_of[d], d), x_recv.at[d, s, d])
            remote(step_refs(s, slot_of[d], d), step_refs(s, 2, d), x_kind(s), x_fwd.at[d, s], x_peer[d]).start()

    def send_sibling(j, s):
        remote(step_refs(s, j), step_refs(s, j, core=1), SIBLING, sib_recv.at[j, s], to_sibling).start()

    def near_x(s):
        for d in range(2):
            arrived(step_refs(s, slot_of[d], 1 - d), x_recv.at[d, s, 1 - d])
            send_sibling(slot_of[d], s)

    def far_x(s):
        for d in range(2):
            arrived(step_refs(s, 2, d), x_fwd.at[d, s])
        send_sibling(2, s)

    def sibling_arrived(s):
        for j in range(4):
            arrived(step_refs(s, j, core=1), sib_recv.at[j, s])

    def send_late(j):
        remote(b_buf.at[j, 0, 0, late_rows], b_buf.at[j, 1, 0, late_rows], Z_LATE, z_late.at[j], to_mirror).start()

    def late_arrived(j):
        arrived(b_buf.at[j, 1, 0, late_rows], z_late.at[j])
        remote(b_buf.at[j, 1, 0, late_rows], b_buf.at[j, 1, 1, late_rows], SIBLING, sib_late.at[j], to_sibling).start()

    def sibling_late_arrived(j):
        arrived(b_buf.at[j, 1, 1, late_rows], sib_late.at[j])

    def send_y(g, part):
        for d in range(2):
            for cc in (d, 1 - d):
                remote(a_buf.at[0, g, cc, part_rows[part]], a_buf.at[slot_of[d], g, cc, part_rows[part]], Y_OWN + part, y_recv.at[d, g, part, cc], y_peer[d]).start()

    def forward_y(g, part):
        for d in range(2):
            got = a_buf.at[slot_of[d], g, d, part_rows[part]]
            arrived(got, y_recv.at[d, g, part, d])
            remote(got, a_buf.at[2, g, d, part_rows[part]], Y_OWN + part, y_fwd.at[d, g, part], y_peer[d]).start()

    def near_y(g, part):
        for d in range(2):
            arrived(a_buf.at[slot_of[d], g, 1 - d, part_rows[part]], y_recv.at[d, g, part, 1 - d])

    def far_y(g, part):
        for d in range(2):
            arrived(a_buf.at[2, g, d, part_rows[part]], y_fwd.at[d, g, part])

    def send_pair(g):
        for cc in range(2):
            remote(a_buf.at[0, (g + 2) % 4, cc, part_rows[0]], a_buf.at[0, g, cc, part_rows[1]], PAIR_A, pair_recv.at[g, cc], to_pair).start()

    def pair_arrived(g):
        for cc in range(2):
            arrived(a_buf.at[0, g, cc, part_rows[1]], pair_recv.at[g, cc])

    def send_pair_full(i):
        remote(a_buf.at[i, 1, :, part_rows[0]], a_buf.at[i, 3, :, part_rows[1]], PAIR_FULL, pair_full.at[i], to_pair).start()

    def pair_full_arrived():
        for i in range(4):
            arrived(a_buf.at[i, 3, :, part_rows[1]], pair_full.at[i])

    def compute(g, part, tiles=(0, 4), slots=(0, 1, 2, 3), by_a=False, add=True, last=False):
        def body(n, carry):
            at = pl.multiple_of(n * tile, tile)
            cols = pl.ds(at, tile)
            total = None
            for slot in slots:
                i, j = (slot, (y + slot - x + 4) % 4) if by_a else ((x + slot - y + 4) % 4, slot)
                for cc in range(2):
                    term = jnp.dot(a_buf[i, g, cc, part_rows[part], :], b_buf[j, g, cc, :, cols], preferred_element_type=jnp.float32)
                    total = term if total is None else total + term
            if add:
                total = total + acc[part_rows[part], cols]
            if not last:
                acc[part_rows[part], cols] = total
            elif part == 1:
                stage[:, cols] = total.astype(stage.dtype)
            else:
                out_ref[:, pl.ds(pl.multiple_of(side * half + at, tile), tile)] = total.astype(out_ref.dtype)
            return carry

        lax.fori_loop(tiles[0], tiles[0] + tiles[1], body, 0)

    def out_cols(of_side, k):
        first, count = C_PIECES[k]
        return pl.ds(pl.multiple_of(of_side * half + first * tile, tile), count * tile)

    def send_c(k):
        first, count = C_PIECES[k]
        remote(stage.at[:, pl.ds(first * tile, count * tile)], out_ref.at[:, out_cols(side, k)], C_KIND, c_recv.at[k], to_pair).start()

    b_load.wait()
    send_x(0)
    remote(b_buf.at[0, 0, 0, early_rows], b_buf.at[0, 1, 0, early_rows], Z_EARLY, z_recv.at[1], to_mirror).start()
    send_late(0)
    a_loaded(0)
    send_y(0, 0)
    a_loaded(2)
    send_pair(0)
    remote(b_ref.at[:, other_cols], b_buf.at[0, 2, 0], Z_KIND, z_recv.at[2], to_pair).start()
    a_loaded(3)
    send_pair(1)
    send_pair(2)
    a_loaded(1)
    send_sibling(0, 0)

    forward_y(0, 0)
    send_y(1, 0)
    send_pair_full(0)
    forward_x(0)
    arrived(step_refs(1, 0), z_recv.at[1])
    send_x(1)
    send_sibling(0, 1)
    near_x(0)
    send_late(3)
    forward_y(1, 0)
    pair_arrived(0)
    send_y(0, 1)
    arrived(b_buf.at[0, 2, 0], z_recv.at[2])
    remote(b_buf.at[0, 2, 0], b_buf.at[0, 3, 0], Z_KIND, z_recv.at[3], to_mirror).start()
    send_x(2)
    send_late(1)
    far_x(0)
    send_late(2)
    send_sibling(0, 2)
    near_y(1, 0)
    send_pair_full(1)
    send_pair_full(3)
    far_y(1, 0)
    send_pair_full(2)
    forward_x(1)
    forward_y(0, 1)
    pair_arrived(1)
    send_y(1, 1)
    near_x(1)
    far_x(1)

    near_y(0, 0)
    far_y(0, 0)
    sibling_arrived(0)
    compute(0, 0, add=False)

    forward_x(2)
    forward_y(1, 1)
    pair_arrived(2)
    send_y(2, 1)
    near_y(0, 1)
    far_y(0, 1)
    compute(0, 1, add=False)

    arrived(b_buf.at[0, 3, 0], z_recv.at[3])
    send_x(3)
    send_x(4)
    for s in (3, 4, 5):
        send_sibling(0, s)
    near_x(2)
    late_arrived(0)
    late_arrived(3)
    forward_y(2, 1)
    send_y(2, 0)
    send_y(3, 0)
    far_x(2)

    forward_x(3)
    send_x(5)
    near_y(1, 1)
    far_y(1, 1)
    late_arrived(1)
    sibling_arrived(1)
    for j in (0, 3, 1):
        sibling_late_arrived(j)
    compute(1, 1, slots=(0, 3, 1))
    forward_y(2, 0)
    near_x(3)
    near_y(2, 1)
    far_y(2, 1)
    sibling_arrived(2)
    compute(2, 1)
    forward_x(4)
    far_x(3)
    late_arrived(2)
    forward_y(3, 0)
    sibling_late_arrived(2)
    compute(1, 1, slots=(2,))
    forward_x(5)
    near_x(4)

    pair_full_arrived()
    sibling_arrived(3)
    compute(3, 1, tiles=(0, 2), last=True)
    send_c(0)
    far_x(4)
    near_x(5)
    sibling_arrived(4)
    compute(3, 1, tiles=(2, 1), last=True)
    send_c(1)
    far_x(5)
    compute(1, 0)
    sibling_arrived(5)
    compute(3, 1, tiles=(3, 1), last=True)
    send_c(2)
    near_y(2, 0)
    far_y(2, 0)
    compute(2, 0)
    near_y(3, 0)
    compute(3, 0, slots=(0, 1, 3), by_a=True)
    far_y(3, 0)
    compute(3, 0, slots=(2,), by_a=True, last=True)

    sent(b_buf.at[pl.ds(0, 3), pl.ds(0, 3), 0], X_KIND)
    sent(b_buf.at[pl.ds(0, 3), 0, 0, early_rows], X_EARLY)
    sent(a_buf.at[pl.ds(0, 3), :, :, part_rows[0]], Y_OWN)
    sent(a_buf.at[pl.ds(0, 3), pl.ds(0, 3), :, part_rows[1]], Y_PAIR)
    sent(a_buf.at[0, pl.ds(0, 3), :, part_rows[0]], PAIR_A)
    sent(a_buf.at[:, 0, :, part_rows[0]], PAIR_FULL)
    sent(b_buf.at[0, pl.ds(0, 2), 0], Z_KIND)
    sent(b_buf.at[0, 0, 0, early_rows], Z_EARLY)
    sent(b_buf.at[:, 0, 0, late_rows], Z_LATE)
    sent(b_buf.at[:, :, 0], SIBLING)
    sent(stage, C_KIND)
    for k in range(len(C_PIECES)):
        arrived(out_ref.at[:, out_cols(1 - side, k)], c_recv.at[k])


def solution(mesh):
    def product(a_blk, b_blk):
        rows, width = a_blk.shape
        half = width // 2
        dma = pltpu.SemaphoreType.DMA
        return pl.pallas_call(
            kernel,
            out_shape=jax.ShapeDtypeStruct((rows, width), jnp.bfloat16),
            in_specs=[pl.BlockSpec(memory_space=pltpu.HBM)] * 2,
            out_specs=pl.BlockSpec(memory_space=pltpu.VMEM),
            scratch_shapes=[
                pltpu.VMEM((4, GROUPS, 2, 2 * rows, rows), jnp.bfloat16),
                pltpu.VMEM((4, GROUPS, 2, rows, half), jnp.bfloat16),
                pltpu.VMEM((2 * rows, half), jnp.float32),
                pltpu.VMEM((rows, half), jnp.bfloat16),
                dma((9,)),
                dma((2, GROUPS, 2, 2)),
                dma((2, GROUPS, 2)),
                dma((GROUPS, 2)),
                dma((4,)),
                dma((2, len(X_STEPS), 2)),
                dma((2, len(X_STEPS))),
                dma((GROUPS,)),
                dma((4,)),
                dma((4, len(X_STEPS))),
                dma((4,)),
                dma((len(C_PIECES),)),
                dma((11,)),
            ],
            compiler_params=pltpu.CompilerParams(collective_id=0, has_side_effects=True, vmem_limit_bytes=56 * 1024 * 1024),
        )(a_blk, b_blk)

    block_spec = P(("row", "depth"), "col")
    return jax.shard_map(product, mesh=mesh, in_specs=(block_spec, block_spec), out_specs=block_spec, check_vma=False)
```

time: 97.3 us -> 82.9 us (0.85)
  Pallas kernels: 93.7 us -> 79.5 us
  local copies, waits for them, and re-layouts: 3.42 us -> 2.3 us
    pallas_call x1, Pallas kernels: 93.7 us -> 79.5 us  [product(): pl.pallas_call(kernel, out_shape=jax.ShapeDtypeStruct((rows, width), jnp....]
    unnamed x5 -> x1, local copies, waits for them, and re-layouts: 3.42 us -> 2.3 us
where the time goes in v3:
time: 82.9 us; the launch traced here: 81.8 us
  Pallas kernels  79.5 us (96%)
  local copies, waits for them, and re-layouts  2.3 us (3%)
    pallas_call x1, Pallas kernels, product(): pl.pallas_call(kernel, out_shape=jax.ShapeDtypeStruct((rows, width), jnp....  79.5 us
    unnamed x1, local copies, waits for them, and re-layouts  2.3 us

profile of v3, /device:TPU:1, one launch (start us, length us, event | category | flops | bytes accessed | tf_op | source)
XLA Modules:
  0.0 81.8 jit_solution(8155153021353187396)
XLA Ops:
  0.0 79.5 %shard_map.28 = bf16[256,2048]{1,0:T(8,128)(2,1)} custom-call(bf16[256,2048]{1,0:T(8,128)(2,1)} %a_ref.1, bf16[256,2048]{1,0:T(8,128)(2,1)} %b_ref.1), custom_call_target="tpu_custom_call" | custom-call | tf_op jit(solution)/shard_map/pallas_call | solution.py:317
  79.5 2.3 %copy.4 = bf16[256,2048]{1,0:T(8,128)(2,1)} copy(bf16[256,2048]{1,0:T(8,128)(2,1)} %shard_map.28) | data formatting | bytes 2097152

commit v4 on v3

--- a/solution.py
+++ b/solution.py
@@ -148,8 +148,7 @@
 
     def compute(g, part, tiles=(0, 4), slots=(0, 1, 2, 3), by_a=False, add=True, last=False):
         def body(n, carry):
-            at = pl.multiple_of(n * tile, tile)
-            cols = pl.ds(at, tile)
+            cols = pl.ds(pl.multiple_of(n * tile, tile), tile)
             total = None
             for slot in slots:
                 i, j = (slot, (y + slot - x + 4) % 4) if by_a else ((x + slot - y + 4) % 4, slot)
@@ -160,10 +159,8 @@
                 total = total + acc[part_rows[part], cols]
             if not last:
                 acc[part_rows[part], cols] = total
-            elif part == 1:
-                stage[:, cols] = total.astype(stage.dtype)
             else:
-                out_ref[:, pl.ds(pl.multiple_of(side * half + at, tile), tile)] = total.astype(out_ref.dtype)
+                stage[part, :, cols] = total.astype(stage.dtype)
             return carry
 
         lax.fori_loop(tiles[0], tiles[0] + tiles[1], body, 0)
@@ -174,7 +171,7 @@
 
     def send_c(k):
         first, count = C_PIECES[k]
-        remote(stage.at[:, pl.ds(first * tile, count * tile)], out_ref.at[:, out_cols(side, k)], C_KIND, c_recv.at[k], to_pair).start()
+        remote(stage.at[1, :, pl.ds(first * tile, count * tile)], out_ref.at[:, out_cols(side, k)], C_KIND, c_recv.at[k], to_pair).start()
 
     b_load.wait()
     send_x(0)
@@ -293,6 +290,8 @@
     compute(3, 0, slots=(0, 1, 3), by_a=True)
     far_y(3, 0)
     compute(3, 0, slots=(2,), by_a=True, last=True)
+    own_out = pltpu.make_async_copy(stage.at[0], out_ref.at[:, my_cols], load_sem.at[9])
+    own_out.start()
 
     sent(b_buf.at[pl.ds(0, 3), pl.ds(0, 3), 0], X_KIND)
     sent(b_buf.at[pl.ds(0, 3), 0, 0, early_rows], X_EARLY)
@@ -304,9 +303,10 @@
     sent(b_buf.at[0, 0, 0, early_rows], Z_EARLY)
     sent(b_buf.at[:, 0, 0, late_rows], Z_LATE)
     sent(b_buf.at[:, :, 0], SIBLING)
-    sent(stage, C_KIND)
+    sent(stage.at[1], C_KIND)
     for k in range(len(C_PIECES)):
         arrived(out_ref.at[:, out_cols(1 - side, k)], c_recv.at[k])
+    own_out.wait()
 
 
 def solution(mesh):
@@ -318,13 +318,13 @@
             kernel,
             out_shape=jax.ShapeDtypeStruct((rows, width), jnp.bfloat16),
             in_specs=[pl.BlockSpec(memory_space=pltpu.HBM)] * 2,
-            out_specs=pl.BlockSpec(memory_space=pltpu.VMEM),
+            out_specs=pl.BlockSpec(memory_space=pl.ANY),
             scratch_shapes=[
                 pltpu.VMEM((4, GROUPS, 2, 2 * rows, rows), jnp.bfloat16),
                 pltpu.VMEM((4, GROUPS, 2, rows, half), jnp.bfloat16),
                 pltpu.VMEM((2 * rows, half), jnp.float32),
-                pltpu.VMEM((rows, half), jnp.bfloat16),
-                dma((9,)),
+                pltpu.VMEM((2, rows, half), jnp.bfloat16),
+                dma((10,)),
                 dma((2, GROUPS, 2, 2)),
                 dma((2, GROUPS, 2)),
                 dma((GROUPS, 2)),
@@ -338,7 +338,7 @@
                 dma((len(C_PIECES),)),
                 dma((11,)),
             ],
-            compiler_params=pltpu.CompilerParams(collective_id=0, has_side_effects=True, vmem_limit_bytes=56 * 1024 * 1024),
+            compiler_params=pltpu.CompilerParams(collective_id=0, has_side_effects=True, vmem_limit_bytes=48 * 1024 * 1024),
         )(a_blk, b_blk)
 
     block_spec = P(("row", "depth"), "col")

time: 82.9 us -> 83.3 us (level)
  local copies, waits for them, and re-layouts: 2.3 us -> 3.42 us
    unnamed x1 -> x5, local copies, waits for them, and re-layouts: 2.3 us -> 3.42 us
where the time goes in v4:
time: 83.3 us; the launch traced here: 82.2 us
  Pallas kernels  78.7 us (94%)
  local copies, waits for them, and re-layouts  3.42 us (4%)
    pallas_call x1, Pallas kernels, product(): pl.pallas_call(kernel, out_shape=jax.ShapeDtypeStruct((rows, width), jnp....  78.7 us
    unnamed x5, local copies, waits for them, and re-layouts  3.42 us

profile of v4, /device:TPU:1, one launch (start us, length us, event | category | flops | bytes accessed | tf_op | source)
XLA Modules:
  0.0 82.2 jit_solution(11248563181397189956)
XLA Ops:
  0.0 0.0 copy-start
  0.0 1.2 %copy-done = bf16[256,2048]{1,0:T(8,128)(2,1)S(1)} copy-done((bf16[256,2048]{1,0:T(8,128)(2,1)S(1)}, bf16[256,2048]{1,0:T(8,128)(2,1)}, u32[]{:S(2)}) %copy-start) | copy-done | bytes 1048600
  1.2 0.0 copy-start.1
  1.2 1.2 %copy-done.1 = bf16[256,2048]{1,0:T(8,128)(2,1)S(1)} copy-done((bf16[256,2048]{1,0:T(8,128)(2,1)S(1)}, bf16[256,2048]{1,0:T(8,128)(2,1)}, u32[]{:S(2)}) %copy-start.1) | copy-done | bytes 1048600
  2.5 78.7 %shard_map.28 = bf16[256,2048]{1,0:T(8,128)(2,1)S(1)} custom-call(bf16[256,2048]{1,0:T(8,128)(2,1)S(1)} %copy-done, bf16[256,2048]{1,0:T(8,128)(2,1)S(1)} %copy-done.1), custom_call_target="tpu_custom_call" | custom-call | tf_op jit(solution)/shard_map/pallas_call | solution.py:317
  81.2 1.0 %copy.4 = bf16[256,2048]{1,0:T(8,128)(2,1)} copy(bf16[256,2048]{1,0:T(8,128)(2,1)S(1)} %shard_map.28) | data formatting | bytes 2097152
Async XLA Ops:
  0.0 1.2 %copy-start = (bf16[256,2048]{1,0:T(8,128)(2,1)S(1)}, bf16[256,2048]{1,0:T(8,128)(2,1)}, u32[]{:S(2)}) copy-start(bf16[256,2048]{1,0:T(8,128)(2,1)} %a_ref.1) | copy-start | bytes 3145732
  1.2 1.2 %copy-start.1 = (bf16[256,2048]{1,0:T(8,128)(2,1)S(1)}, bf16[256,2048]{1,0:T(8,128)(2,1)}, u32[]{:S(2)}) copy-start(bf16[256,2048]{1,0:T(8,128)(2,1)} %b_ref.1) | copy-start | bytes 3145732

commit v5 on v3

--- a/solution.py
+++ b/solution.py
@@ -316,7 +316,7 @@
         dma = pltpu.SemaphoreType.DMA
         return pl.pallas_call(
             kernel,
-            out_shape=jax.ShapeDtypeStruct((rows, width), jnp.bfloat16),
+            out_shape=pltpu.VMEM((rows, width), jnp.bfloat16),
             in_specs=[pl.BlockSpec(memory_space=pltpu.HBM)] * 2,
             out_specs=pl.BlockSpec(memory_space=pltpu.VMEM),
             scratch_shapes=[

time: 82.9 us -> 80.5 us (0.971)
  local copies, waits for them, and re-layouts: 2.3 us -> 0.97 us
  Pallas kernels: 79.5 us -> 78.5 us
    unnamed x1, local copies, waits for them, and re-layouts: 2.3 us -> 0.97 us
    pallas_call x1, Pallas kernels: 79.5 us -> 78.5 us  [product(): pl.pallas_call(kernel, out_shape=pltpu.VMEM((rows, width), jnp.bfloat16),...]
where the time goes in v5:
time: 80.5 us; the launch traced here: 79.5 us
  Pallas kernels  78.5 us (98%)
  local copies, waits for them, and re-layouts  0.97 us (1%)
    pallas_call x1, Pallas kernels, product(): pl.pallas_call(kernel, out_shape=pltpu.VMEM((rows, width), jnp.bfloat16),...  78.5 us

profile of v5, /device:TPU:1, one launch (start us, length us, event | category | flops | bytes accessed | tf_op | source)
XLA Modules:
  0.0 79.5 jit_solution(5760518905959796217)
XLA Ops:
  0.0 78.5 %shard_map.28 = bf16[256,2048]{1,0:T(8,128)(2,1)S(1)} custom-call(bf16[256,2048]{1,0:T(8,128)(2,1)} %a_ref.1, bf16[256,2048]{1,0:T(8,128)(2,1)} %b_ref.1), custom_call_target="tpu_custom_call" | custom-call | tf_op jit(solution)/shard_map/pallas_call | solution.py:317
  78.5 1.0 %copy.4 = bf16[256,2048]{1,0:T(8,128)(2,1)} copy(bf16[256,2048]{1,0:T(8,128)(2,1)S(1)} %shard_map.28) | data formatting | bytes 2097152

commit v6 on v5

--- a/solution.py
+++ b/solution.py
@@ -49,6 +49,9 @@
         start = pl.multiple_of(which * half + z_of[g] * rows, rows)
         return pltpu.make_async_copy(a_ref.at[:, pl.ds(start, rows)], a_buf.at[0, g, cc, part_rows[0]], load_sem.at[g * 2 + cc])
 
+    def b_loaded():
+        b_load.wait()
+
     def a_loaded(g):
         for cc in range(2):
             a_load(g, cc).wait()
@@ -145,6 +148,18 @@
     def pair_full_arrived():
         for i in range(4):
             arrived(a_buf.at[i, 3, :, part_rows[1]], pair_full.at[i])
+
+    def send_z_early():
+        remote(b_buf.at[0, 0, 0, early_rows], b_buf.at[0, 1, 0, early_rows], Z_EARLY, z_recv.at[1], to_mirror).start()
+
+    def send_z_pair():
+        remote(b_ref.at[:, other_cols], b_buf.at[0, 2, 0], Z_KIND, z_recv.at[2], to_pair).start()
+
+    def send_z_mirror():
+        remote(b_buf.at[0, 2, 0], b_buf.at[0, 3, 0], Z_KIND, z_recv.at[3], to_mirror).start()
+
+    def z_arrived(g):
+        arrived(b_buf.at[0, g, 0, early_rows] if g == 1 else b_buf.at[0, g, 0], z_recv.at[g])
 
     def compute(g, part, tiles=(0, 4), slots=(0, 1, 2, 3), by_a=False, add=True, last=False):
         def body(n, carry):
@@ -176,116 +191,114 @@
         first, count = C_PIECES[k]
         remote(stage.at[:, pl.ds(first * tile, count * tile)], out_ref.at[:, out_cols(side, k)], C_KIND, c_recv.at[k], to_pair).start()
 
-    b_load.wait()
+    b_loaded()
     send_x(0)
-    remote(b_buf.at[0, 0, 0, early_rows], b_buf.at[0, 1, 0, early_rows], Z_EARLY, z_recv.at[1], to_mirror).start()
+    send_z_early()
     send_late(0)
     a_loaded(0)
     send_y(0, 0)
     a_loaded(2)
     send_pair(0)
-    remote(b_ref.at[:, other_cols], b_buf.at[0, 2, 0], Z_KIND, z_recv.at[2], to_pair).start()
+    send_z_pair()
     a_loaded(3)
     send_pair(1)
     send_pair(2)
     a_loaded(1)
+    send_pair_full(0)
     send_sibling(0, 0)
 
     forward_y(0, 0)
     send_y(1, 0)
-    send_pair_full(0)
-    forward_x(0)
-    arrived(step_refs(1, 0), z_recv.at[1])
+    z_arrived(1)
     send_x(1)
     send_sibling(0, 1)
+    forward_x(0)
     near_x(0)
     send_late(3)
     forward_y(1, 0)
     pair_arrived(0)
     send_y(0, 1)
-    arrived(b_buf.at[0, 2, 0], z_recv.at[2])
-    remote(b_buf.at[0, 2, 0], b_buf.at[0, 3, 0], Z_KIND, z_recv.at[3], to_mirror).start()
-    send_x(2)
-    send_late(1)
-    far_x(0)
-    send_late(2)
-    send_sibling(0, 2)
+    forward_x(1)
     near_y(1, 0)
     send_pair_full(1)
     send_pair_full(3)
+    z_arrived(2)
+    send_z_mirror()
+    send_x(2)
+    send_late(1)
+    send_sibling(0, 2)
+    far_x(0)
+    send_late(2)
     far_y(1, 0)
     send_pair_full(2)
-    forward_x(1)
+    near_x(1)
+    near_y(0, 0)
+    far_y(0, 0)
     forward_y(0, 1)
+    sibling_arrived(0)
+    compute(0, 0, add=False)
     pair_arrived(1)
     send_y(1, 1)
-    near_x(1)
     far_x(1)
-
-    near_y(0, 0)
-    far_y(0, 0)
-    sibling_arrived(0)
-    compute(0, 0, add=False)
-
+    near_y(0, 1)
+    far_y(0, 1)
+    compute(0, 1, add=False)
     forward_x(2)
     forward_y(1, 1)
     pair_arrived(2)
     send_y(2, 1)
-    near_y(0, 1)
-    far_y(0, 1)
-    compute(0, 1, add=False)
-
-    arrived(b_buf.at[0, 3, 0], z_recv.at[3])
+    late_arrived(0)
+    late_arrived(3)
+    sibling_arrived(1)
+    for j in (0, 3):
+        sibling_late_arrived(j)
+    compute(1, 0, slots=(0, 3))
+    near_x(2)
+    z_arrived(3)
     send_x(3)
     send_x(4)
     for s in (3, 4, 5):
         send_sibling(0, s)
-    near_x(2)
-    late_arrived(0)
-    late_arrived(3)
+    near_y(1, 1)
+    far_y(1, 1)
+    compute(1, 1, slots=(0, 3))
     forward_y(2, 1)
     send_y(2, 0)
     send_y(3, 0)
     far_x(2)
-
     forward_x(3)
     send_x(5)
-    near_y(1, 1)
-    far_y(1, 1)
-    late_arrived(1)
-    sibling_arrived(1)
-    for j in (0, 3, 1):
-        sibling_late_arrived(j)
-    compute(1, 1, slots=(0, 3, 1))
-    forward_y(2, 0)
-    near_x(3)
     near_y(2, 1)
     far_y(2, 1)
     sibling_arrived(2)
     compute(2, 1)
+    near_x(3)
+    late_arrived(1)
+    forward_y(2, 0)
     forward_x(4)
+    near_x(4)
+    sibling_late_arrived(1)
+    compute(1, 1, slots=(1,))
     far_x(3)
     late_arrived(2)
+    forward_x(5)
     forward_y(3, 0)
+    pair_full_arrived()
     sibling_late_arrived(2)
     compute(1, 1, slots=(2,))
-    forward_x(5)
-    near_x(4)
-
-    pair_full_arrived()
     sibling_arrived(3)
     compute(3, 1, tiles=(0, 2), last=True)
     send_c(0)
+    near_x(5)
     far_x(4)
-    near_x(5)
     sibling_arrived(4)
     compute(3, 1, tiles=(2, 1), last=True)
     send_c(1)
     far_x(5)
-    compute(1, 0)
     sibling_arrived(5)
     compute(3, 1, tiles=(3, 1), last=True)
     send_c(2)
+    compute(1, 0, slots=(1, 2))
     near_y(2, 0)
     far_y(2, 0)
     compute(2, 0)

time: 80.5 us -> 77.8 us (0.966); the launches traced: 79.5 us -> 77.7 us
  Pallas kernels: 78.5 us -> 76.7 us
    pallas_call x1, Pallas kernels: 78.5 us -> 76.7 us  [product(): pl.pallas_call(kernel, out_shape=pltpu.VMEM((rows, width), jnp.bfloat16),...]
where the time goes in v6:
time: 77.8 us; the launch traced here: 77.7 us
  Pallas kernels  76.7 us (99%)
  local copies, waits for them, and re-layouts  0.97 us (1%)
    pallas_call x1, Pallas kernels, product(): pl.pallas_call(kernel, out_shape=pltpu.VMEM((rows, width), jnp.bfloat16),...  76.7 us

profile of v6, /device:TPU:1, one launch (start us, length us, event | category | flops | bytes accessed | tf_op | source)
XLA Modules:
  0.0 77.7 jit_solution(9946779735486543402)
XLA Ops:
  0.0 76.7 %shard_map.28 = bf16[256,2048]{1,0:T(8,128)(2,1)S(1)} custom-call(bf16[256,2048]{1,0:T(8,128)(2,1)} %a_ref.1, bf16[256,2048]{1,0:T(8,128)(2,1)} %b_ref.1), custom_call_target="tpu_custom_call" | custom-call | tf_op jit(solution)/shard_map/pallas_call | solution.py:330
  76.7 1.0 %copy.4 = bf16[256,2048]{1,0:T(8,128)(2,1)} copy(bf16[256,2048]{1,0:T(8,128)(2,1)S(1)} %shard_map.28) | data formatting | bytes 2097152

commit v7 on v0

v7 whole, which is shorter than its diff:
```python
import jax
import jax.numpy as jnp
from jax import lax
from jax.experimental import pallas as pl
from jax.experimental.pallas import tpu as pltpu
from jax.sharding import PartitionSpec as P

MESH = pl.DeviceIdType.MESH
GROUPS = 4
UNITS = 8
ALL, OUTER, INNER, NEAR, FAR = (0, 1, 2, 3), (0, 3), (1, 2), (0, 1, 3), (2,)
X_STEPS = ((0, False, 0, 8), (1, True, 0, 8), (2, False, 0, 8), (3, False, 0, 2), (3, False, 2, 2), (3, False, 4, 2), (3, False, 6, 1), (3, False, 7, 1))
STEPS = range(len(X_STEPS))
LAST_STEPS = [s for s in STEPS if X_STEPS[s][0] == 3]
Y_STEPS = ((0, 0), (1, 0), (0, 1), (1, 1), (2, 1), (3, 1), (2, 0), (3, 0))
LATE = ((0, 0), (0, 1), (3, 0), (3, 1), (1, 0), (2, 0), (1, 1), (2, 1))
PRODUCTS = (
    (0, 0, 4, 4, ALL),
    (0, 1, 4, 4, ALL),
    (0, 0, 0, 4, ALL),
    (0, 1, 0, 4, ALL),
    (1, 0, 0, 4, OUTER),
    (1, 0, 4, 4, OUTER),
    (1, 1, 4, 4, OUTER),
    (2, 1, 0, 4, ALL),
    (1, 1, 0, 4, OUTER),
    (1, 1, 0, 4, INNER),
    (1, 0, 0, 4, INNER),
    (3, 1, 0, 2, ALL),
    (2, 1, 4, 4, ALL),
    (3, 1, 2, 2, ALL),
    (1, 1, 4, 4, INNER),
    (3, 1, 4, 2, ALL),
    (1, 0, 4, 4, INNER),
    (3, 1, 6, 1, ALL),
    (2, 0, 4, 4, ALL),
    (3, 1, 7, 1, ALL),
    (2, 0, 0, 4, ALL),
    (3, 0, 0, 8, NEAR),
    (3, 0, 0, 8, FAR),
)
X_KIND, X_EARLY, Y_OWN, Y_PAIR, Y_LAST, PAIR_A, PAIR_LAST, FULL, FULL_LAST, Z_KIND, Z_EARLY, Z_LATE, SIBLING, C_KIND = range(14)


def stepper(function, order):
    entries = iter(order)

    def step():
        entry = next(entries)
        function(*(entry if isinstance(entry, tuple) else (entry,)))

    return step


def kernel(a_ref, b_ref, out_ref, a_buf, b_buf, acc, stage, load_sem, y_recv, y_fwd, pair_recv, pair_full, x_recv, x_fwd, z_recv, z_late, sib_recv, sib_late, c_recv, send_sem):
    z, y, r = lax.axis_index("depth"), lax.axis_index("col"), lax.axis_index("row")
    x, c = r // 2, r % 2
    rows, width = a_ref.shape
    half = width // 2
    unit = half // UNITS
    early = rows // 4
    over_y = rows * 3 // 8

    pair = z + 1 - 2 * (z % 2)
    mirror = 3 - z
    side = ((z + 1) // 2) % 2
    z_of = (z, mirror, pair, 3 - pair)

    y_peer = ({"col": (y + 1) % 4}, {"col": (y + 3) % 4})
    x_peer = ({"row": ((x + 1) % 4) * 2 + c}, {"row": ((x + 3) % 4) * 2 + c})
    to_pair, to_mirror, to_sibling = {"depth": pair}, {"depth": mirror}, {"row": x * 2 + 1 - c}
    peers = y_peer + x_peer + (to_pair, to_mirror, to_sibling)
    both = range(2)

    def remote(src, dst, kind, recv, where):
        return pltpu.make_async_remote_copy(src_ref=src, dst_ref=dst, send_sem=send_sem.at[kind], recv_sem=recv, device_id=where, device_id_type=MESH)

    waited = set()

    def arrived(ref, recv, *key):
        if key not in waited:
            waited.add(key)
            remote(ref, ref, X_KIND, recv, to_sibling).wait_recv()

    def sent(ref, kind):
        remote(ref, ref, kind, c_recv, to_sibling).wait_send()

    own_rows, pair_rows = part_rows = (pl.ds(0, rows), pl.ds(rows, rows))
    early_rows, late_rows = pl.ds(0, early), pl.ds(early, rows - early)
    col_half = (pl.ds(0, half // 2), pl.ds(half // 2, half // 2))
    my_cols = pl.ds(pl.multiple_of(side * half, half), half)
    other_cols = pl.ds(pl.multiple_of((1 - side) * half, half), half)
    slot_of = (3, 1)

    b_load = pltpu.make_async_copy(b_ref.at[:, my_cols], b_buf.at[0, 0, 0], load_sem.at[GROUPS])
    b_load.start()
    for g in (0, 2, 3, 1):
        for cc in both:
            start = pl.multiple_of((c + cc - 2 * c * cc) * half + z_of[g] * rows, rows)
            pltpu.make_async_copy(a_ref.at[:, pl.ds(start, rows)], a_buf.at[0, g, cc, own_rows], load_sem.at[g]).start()

    barrier = pltpu.get_barrier_semaphore()
    for where in peers:
        pl.semaphore_signal(barrier, inc=1, device_id=where, device_id_type=MESH)
    pl.semaphore_wait(barrier, len(peers))

    def loaded(g):
        arrived(a_buf.at[0, g, :, own_rows], load_sem.at[g], "load", g)

    def x_ref(s, slot, piece=None, core=0):
        g, early_only, first, count = X_STEPS[s]
        size = early if early_only else rows
        at = pl.ds(0, size) if piece is None else pl.ds(piece * (size // 2), size // 2)
        return b_buf.at[slot, g, core, at, pl.ds(first * unit, count * unit)]

    def x_kind(s):
        return X_EARLY if X_STEPS[s][1] else X_KIND

    def x_got(s, n):
        arrived(x_ref(s, 1), x_recv.at[s, n], "x", s, n)

    def far_x_got(s):
        arrived(x_ref(s, 2), x_fwd.at[s], "fx", s)

    def z_got(g):
        if g > 0:
            arrived(b_buf.at[0, g, 0, early_rows] if g == 1 else b_buf.at[0, g, 0], z_recv.at[g - 1], "z", g)

    @lambda f: stepper(f, [(s, n) for s in STEPS for n in both])
    def send_x(s, n):
        z_got(X_STEPS[s][0])
        for d in both:
            h = (d + n) % 2
            remote(x_ref(s, 0, h), x_ref(s, slot_of[d], h), x_kind(s), x_recv.at[s, n], x_peer[d]).start()

    @lambda f: stepper(f, STEPS)
    def forward_x(s):
        x_got(s, 0)
        for d in both:
            remote(x_ref(s, slot_of[d], d), x_ref(s, 2, d), x_kind(s), x_fwd.at[s], x_peer[d]).start()

    def send_sibling(s, j):
        remote(x_ref(s, j), x_ref(s, j, core=1), SIBLING, sib_recv.at[s], to_sibling).start()

    @lambda f: stepper(f, STEPS)
    def sib_own(s):
        z_got(X_STEPS[s][0])
        send_sibling(s, 0)

    @lambda f: stepper(f, STEPS)
    def sib_near(s):
        x_got(s, 0)
        x_got(s, 1)
        for slot in slot_of:
            send_sibling(s, slot)

    @lambda f: stepper(f, STEPS)
    def sib_far(s):
        far_x_got(s)
        send_sibling(s, 2)

    def sibling_got(s):
        arrived(x_ref(s, slice(None), core=1), sib_recv.at[s], "sib", s)

    def send_z_early():
        remote(b_buf.at[0, 0, 0, early_rows], b_buf.at[0, 1, 0, early_rows], Z_EARLY, z_recv.at[0], to_mirror).start()

    def send_z_pair():
        remote(b_ref.at[:, other_cols], b_buf.at[0, 2, 0], Z_KIND, z_recv.at[1], to_pair).start()

    def send_z_mirror():
        z_got(2)
        remote(b_buf.at[0, 2, 0], b_buf.at[0, 3, 0], Z_KIND, z_recv.at[2], to_mirror).start()

    def late_ref(j, k, g=1, core=0):
        return b_buf.at[j, g, core, late_rows, col_half[k]]

    def late_got(j, k):
        arrived(late_ref(j, k), z_late.at[j, k], "late", j, k)

    @lambda f: stepper(f, LATE)
    def send_late(j, k):
        if j == 2:
            far_x_got(0)
        elif j > 0:
            x_got(0, 0)
            x_got(0, 1)
        remote(late_ref(j, k, 0), late_ref(j, k), Z_LATE, z_late.at[j, k], to_mirror).start()

    @lambda f: stepper(f, LATE)
    def late_sibling(j, k):
        late_got(j, k)
        remote(late_ref(j, k), late_ref(j, k, core=1), SIBLING, sib_late.at[int(j in INNER), k], to_sibling).start()

    def late_sibling_got(slots, k):
        arrived(late_ref(pl.ds(0, 2), k, core=1), sib_late.at[int(slots == INNER), k], "sl", slots, k)

    first_rows, second_rows = pl.ds(rows, over_y), pl.ds(rows + over_y, rows - over_y)
    first_own, second_own = pl.ds(0, over_y), pl.ds(over_y, rows - over_y)

    def y_piece(slot, g, part, h):
        if (g, part) == (3, 1):
            return a_buf.at[slot, g, 1, pl.ds(rows + h * (over_y // 2), over_y // 2)]
        return a_buf.at[slot, g, h, part_rows[part]]

    def y_whole(g, part):
        return a_buf.at[1, g, 1, first_rows] if (g, part) == (3, 1) else a_buf.at[1, g, :, part_rows[part]]

    def y_kind(g, part):
        return Y_LAST if (g, part) == (3, 1) else Y_OWN + part

    def y_got(g, part, n):
        arrived(y_whole(g, part), y_recv.at[g, part, n], "y", g, part, n)

    def far_y_got(g, part):
        arrived(y_whole(g, part), y_fwd.at[g, part], "fy", g, part)

    def pair_got(g):
        arrived(a_buf.at[0, g, :, pair_rows] if g < 3 else a_buf.at[0, 3, 1, first_rows], pair_recv.at[g], "pair", g)

    @lambda f: stepper(f, [(g, part, n) for g, part in Y_STEPS for n in both])
    def send_y(g, part, n):
        if part == 1:
            pair_got(g)
        else:
            loaded(g)
        for d in both:
            h = (d + n) % 2
            remote(y_piece(0, g, part, h), y_piece(slot_of[d], g, part, h), y_kind(g, part), y_recv.at[g, part, n], y_peer[d]).start()

    @lambda f: stepper(f, Y_STEPS)
    def forward_y(g, part):
        y_got(g, part, 0)
        for d in both:
            remote(y_piece(slot_of[d], g, part, d), y_piece(2, g, part, d), y_kind(g, part), y_fwd.at[g, part], y_peer[d]).start()

    @lambda f: stepper(f, range(GROUPS))
    def send_pair(g):
        loaded((g + 2) % 4)
        if g < 3:
            remote(a_buf.at[0, (g + 2) % 4, :, own_rows], a_buf.at[0, g, :, pair_rows], PAIR_A, pair_recv.at[g], to_pair).start()
        else:
            remote(a_buf.at[0, 1, 1, first_own], a_buf.at[0, 3, 1, first_rows], PAIR_LAST, pair_recv.at[3], to_pair).start()

    @lambda f: stepper(f, (0, 1, 3, 2))
    def send_full(i):
        if i == 0:
            loaded(1)
        elif i == 2:
            far_y_got(1, 0)
        else:
            y_got(1, 0, 0)
            y_got(1, 0, 1)
        remote(a_buf.at[i, 1, 0, own_rows], a_buf.at[i, 3, 0, pair_rows], FULL, pair_full.at[0], to_pair).start()
        remote(a_buf.at[i, 1, 1, second_own], a_buf.at[i, 3, 1, second_rows], FULL_LAST, pair_full.at[1], to_pair).start()

    def full_got():
        arrived(a_buf.at[:, 3, 0, pair_rows], pair_full.at[0], "full", 0)
        arrived(a_buf.at[:, 3, 1, second_rows], pair_full.at[1], "full", 1)

    def ready(g, part, first, count, slots):
        if part == 0:
            loaded(g)
        else:
            pair_got(g)
        if (g, part) == (3, 1):
            full_got()
        if slots != FAR:
            y_got(g, part, 0)
            y_got(g, part, 1)
        if slots != NEAR:
            far_y_got(g, part)
        z_got(g)
        for s in STEPS:
            step_group, _, step_first, step_count = X_STEPS[s]
            if step_group == g and step_first < first + count and first < step_first + step_count:
                x_got(s, 0)
                x_got(s, 1)
                far_x_got(s)
                sibling_got(s)
        if g == 1:
            for j in slots:
                late_got(j, first * 2 // UNITS)
            late_sibling_got(slots, first * 2 // UNITS)

    @lambda f: stepper(f, PRODUCTS)
    def compute(g, part, first, count, slots):
        ready(g, part, first, count, slots)
        by_a = slots in (NEAR, FAR)
        last = g == 3 and slots != NEAR
        add = g > 0
        size = min(count, 2) * unit

        def body(n, carry=0):
            at = first * unit + n * size
            cols = pl.ds(at if isinstance(n, int) else pl.multiple_of(at, size), size)
            total = None
            for slot in slots:
                i, j = (slot, (y + slot - x + 4) % 4) if by_a else ((x + slot - y + 4) % 4, slot)
                for cc in both:
                    term = jnp.dot(a_buf[i, g, cc, part_rows[part], :], b_buf[j, g, cc, :, cols], preferred_element_type=jnp.float32)
                    total = term if total is None else total + term
            if add:
                total = total + acc[part_rows[part], cols]
            if not last:
                acc[part_rows[part], cols] = total
            elif part == 1:
                stage[:, cols] = total.astype(stage.dtype)
            else:
                out_ref[:, pl.ds(pl.multiple_of(side * half + at, size), size)] = total.astype(out_ref.dtype)
            return carry

        if count <= 2 or slots == FAR:
            for n in range((count + 1) // 2):
                body(n)
        else:
            lax.fori_loop(0, count // 2, body, 0)

    @lambda f: stepper(f, LAST_STEPS)
    def send_c(s):
        _, _, first, count = X_STEPS[s]
        at = pl.ds(pl.multiple_of(side * half + first * unit, unit), count * unit)
        remote(stage.at[:, pl.ds(first * unit, count * unit)], out_ref.at[:, at], C_KIND, c_recv, to_pair).start()

    b_load.wait()
    send_pair()
    send_y()
    send_x()
    send_x()
    send_z_pair()
    send_z_early()
    send_pair()
    send_y()
    send_y()
    send_late()
    send_y()
    send_pair()
    send_x()
    send_x()
    forward_x()
    send_late()
    forward_y()
    sib_own()
    send_y()
    late_sibling()
    send_y()
    sib_near()
    send_late()
    forward_y()
    send_late()
    sib_near()
    sib_own()
    send_z_mirror()
    send_x()
    forward_y()
    send_pair()
    send_y()
    send_late()
    sib_far()
    send_x()
    send_y()
    send_full()
    forward_x()
    forward_x()
    send_full()
    late_sibling()
    send_y()
    send_y()
    late_sibling()
    send_y()
    sib_own()
    send_late()
    compute()
    send_full()
    compute()
    compute()
    sib_own()
    forward_y()
    late_sibling()
    sib_own()
    send_x()
    send_x()
    send_x()
    compute()
    send_late()
    forward_y()
    send_x()
    sib_far()
    sib_far()
    send_y()
    send_y()
    sib_near()
    send_late()
    compute()
    forward_x()
    send_x()
    send_full()
    late_sibling()
    sib_near()
    compute()
    compute()
    forward_y()
    forward_x()
    send_y()
    late_sibling()
    send_y()
    compute()
    compute()
    sib_own()
    send_x()
    compute()
    send_x()
    sib_far()
    sib_near()
    forward_y()
    forward_x()
    compute()
    send_x()
    send_x()
    compute()
    send_c()
    sib_far()
    late_sibling()
    compute()
    compute()
    late_sibling()
    sib_near()
    forward_x()
    send_c()
    sib_far()
    send_y()
    send_x()
    compute()
    forward_x()
    sib_own()
    compute()
    sib_near()
    send_c()
    sib_own()
    forward_y()
    compute()
    sib_far()
    sib_near()
    compute()
    send_c()
    sib_far()
    compute()
    compute()
    send_c()
    compute()
    compute()
    compute()

    sent(b_buf.at[pl.ds(0, 3), pl.ds(0, 3), 0], X_KIND)
    sent(b_buf.at[pl.ds(0, 3), 0, 0, early_rows], X_EARLY)
    sent(a_buf.at[pl.ds(0, 3), :, :, own_rows], Y_OWN)
    sent(a_buf.at[pl.ds(0, 3), pl.ds(0, 3), :, pair_rows], Y_PAIR)
    sent(a_buf.at[pl.ds(0, 3), 3, 1, first_rows], Y_LAST)
    sent(a_buf.at[0, pl.ds(0, 3), :, own_rows], PAIR_A)
    sent(a_buf.at[0, 3, 1, first_rows], PAIR_LAST)
    sent(a_buf.at[:, 0, 0, own_rows], FULL)
    sent(a_buf.at[:, 3, 1, second_rows], FULL_LAST)
    sent(b_buf.at[0, pl.ds(0, 2), 0], Z_KIND)
    sent(b_buf.at[0, 0, 0, early_rows], Z_EARLY)
    sent(b_buf.at[:, 0, 0, late_rows], Z_LATE)
    sent(b_buf.at[:, :, 0], SIBLING)
    sent(stage, C_KIND)
    arrived(out_ref.at[:, other_cols], c_recv, "c")


def solution(mesh):
    def product(a_blk, b_blk):
        rows, width = a_blk.shape
        half = width // 2
        dma = pltpu.SemaphoreType.DMA
        return pl.pallas_call(
            kernel,
            out_shape=pltpu.VMEM((rows, width), jnp.bfloat16),
            in_specs=[pl.BlockSpec(memory_space=pltpu.HBM)] * 2,
            out_specs=pl.BlockSpec(memory_space=pltpu.VMEM),
            scratch_shapes=[
                pltpu.VMEM((4, GROUPS, 2, 2 * rows, rows), jnp.bfloat16),
                pltpu.VMEM((4, GROUPS, 2, rows, half), jnp.bfloat16),
                pltpu.VMEM((2 * rows, half), jnp.float32),
                pltpu.VMEM((rows, half), jnp.bfloat16),
                dma((GROUPS + 1,)),
                dma((GROUPS, 2, 2)),
                dma((GROUPS, 2)),
                dma((GROUPS,)),
                dma((2,)),
                dma((len(X_STEPS), 2)),
                dma((len(X_STEPS),)),
                dma((3,)),
                dma((4, 2)),
                dma((len(X_STEPS),)),
                dma((2, 2)),
                dma(()),
                dma((14,)),
            ],
            compiler_params=pltpu.CompilerParams(collective_id=0, has_side_effects=True, vmem_limit_bytes=56 * 1024 * 1024),
        )(a_blk, b_blk)

    block_spec = P(("row", "depth"), "col")
    return jax.shard_map(product, mesh=mesh, in_specs=(block_spec, block_spec), out_specs=block_spec, check_vma=False)
```

time: 409 us -> 72.8 us (0.18); the launches traced: 404 us -> 72.7 us
  waiting for transfers between devices: 298 us -> 0 us
  starting transfers between devices: 71.8 us -> 0 us
  Pallas kernels: 0 us -> 71.7 us
  matrix products: 15.3 us -> 0 us
  between operations: 13.1 us -> 0.01 us
  other arithmetic: 6.33 us -> 0 us
    reduce_scatter x1 -> x0, waiting for transfers between devices: 139 us -> none  [local_product(): lax.psum_scatter(part_sum, 'depth', scatter_dimension=0, tiled=True)]
    ppermute x4 -> x0, waiting for transfers between devices: 87.7 us -> none  [the longest x1 87.7 us: local_product(): a_tail = lax.ppermute(a_full, all_axes, a_after)]
    ppermute x4 -> x0, starting transfers between devices: 71.7 us -> none  [the longest x1 33.1 us: local_product(): a_lead = lax.ppermute(a_full, all_axes, a_start)]
    pallas_call x0 -> x1, Pallas kernels: none -> 71.7 us  [product(): pl.pallas_call(kernel, out_shape=pltpu.VMEM((rows, width), jnp.bfloat16),...]
    all_gather x2 -> x0, waiting for transfers between devices: 69.4 us -> none  [the longest x1 52.2 us: local_product(): b_full = lax.all_gather(b_blk, 'depth', axis=0, tiled=True)]
    dot_general x2 -> x0, matrix products: 15.3 us -> none  [the longest x1 9.03 us: local_product(): jnp.dot(pieces[0], b_cur, preferred_element_type=jnp.float32)]
  transfers between devices with their start and end apart: 7 -> 0, of which waited for: 4 -> 0; matrix products, arithmetic and copies ran while one was open for 2% -> 0% of each run, Pallas kernels for 0% -> 0%
where the time goes in v7:
time: 72.8 us; the launch traced here: 72.7 us
  Pallas kernels  71.7 us (98%)
  local copies, waits for them, and re-layouts  0.97 us (1%)
    pallas_call x1, Pallas kernels, product(): pl.pallas_call(kernel, out_shape=pltpu.VMEM((rows, width), jnp.bfloat16),...  71.7 us

profile of v7, /device:TPU:1, one launch (start us, length us, event | category | flops | bytes accessed | tf_op | source)
XLA Modules:
  0.0 72.7 jit_solution(188063182660485487)
XLA Ops:
  0.0 71.7 %shard_map.28 = bf16[256,2048]{1,0:T(8,128)(2,1)S(1)} custom-call(bf16[256,2048]{1,0:T(8,128)(2,1)} %a_ref.1, bf16[256,2048]{1,0:T(8,128)(2,1)} %b_ref.1), custom_call_target="tpu_custom_call" | custom-call | tf_op jit(solution)/shard_map/pallas_call | solution.py:476
  71.7 1.0 %copy.4 = bf16[256,2048]{1,0:T(8,128)(2,1)} copy(bf16[256,2048]{1,0:T(8,128)(2,1)S(1)} %shard_map.28) | data formatting | bytes 2097152

commit v8 on v7

--- a/solution.py
+++ b/solution.py
@@ -39,7 +39,7 @@
     (3, 0, 0, 8, NEAR),
     (3, 0, 0, 8, FAR),
 )
-X_KIND, X_EARLY, Y_OWN, Y_PAIR, Y_LAST, PAIR_A, PAIR_LAST, FULL, FULL_LAST, Z_KIND, Z_EARLY, Z_LATE, SIBLING, C_KIND = range(14)
+BIG, SMALL = range(2)
 
 
 def stepper(function, order):
@@ -80,7 +80,7 @@
     def arrived(ref, recv, *key):
         if key not in waited:
             waited.add(key)
-            remote(ref, ref, X_KIND, recv, to_sibling).wait_recv()
+            remote(ref, ref, BIG, recv, to_sibling).wait_recv()
 
     def sent(ref, kind):
         remote(ref, ref, kind, c_recv, to_sibling).wait_send()
@@ -92,20 +92,20 @@
     other_cols = pl.ds(pl.multiple_of((1 - side) * half, half), half)
     slot_of = (3, 1)
 
-    b_load = pltpu.make_async_copy(b_ref.at[:, my_cols], b_buf.at[0, 0, 0], load_sem.at[GROUPS])
+    b_load = pltpu.make_async_copy(b_ref.at[:, my_cols], b_buf.at[0, 0, 0], load_sem.at[1])
     b_load.start()
-    for g in (0, 2, 3, 1):
+    for g in range(GROUPS):
         for cc in both:
             start = pl.multiple_of((c + cc - 2 * c * cc) * half + z_of[g] * rows, rows)
-            pltpu.make_async_copy(a_ref.at[:, pl.ds(start, rows)], a_buf.at[0, g, cc, own_rows], load_sem.at[g]).start()
+            pltpu.make_async_copy(a_ref.at[:, pl.ds(start, rows)], a_buf.at[0, g, cc, own_rows], load_sem.at[0]).start()
 
     barrier = pltpu.get_barrier_semaphore()
     for where in peers:
         pl.semaphore_signal(barrier, inc=1, device_id=where, device_id_type=MESH)
     pl.semaphore_wait(barrier, len(peers))
 
-    def loaded(g):
-        arrived(a_buf.at[0, g, :, own_rows], load_sem.at[g], "load", g)
+    def loaded():
+        arrived(a_buf.at[0, :, :, own_rows], load_sem.at[0], "load")
 
     def x_ref(s, slot, piece=None, core=0):
         g, early_only, first, count = X_STEPS[s]
@@ -114,7 +114,7 @@
         return b_buf.at[slot, g, core, at, pl.ds(first * unit, count * unit)]
 
     def x_kind(s):
-        return X_EARLY if X_STEPS[s][1] else X_KIND
+        return SMALL if X_STEPS[s][1] else BIG
 
     def x_got(s, n):
         arrived(x_ref(s, 1), x_recv.at[s, n], "x", s, n)
@@ -140,7 +140,7 @@
             remote(x_ref(s, slot_of[d], d), x_ref(s, 2, d), x_kind(s), x_fwd.at[s], x_peer[d]).start()
 
     def send_sibling(s, j):
-        remote(x_ref(s, j), x_ref(s, j, core=1), SIBLING, sib_recv.at[s], to_sibling).start()
+        remote(x_ref(s, j), x_ref(s, j, core=1), BIG, sib_recv.at[s], to_sibling).start()
 
     @lambda f: stepper(f, STEPS)
     def sib_own(s):
@@ -163,14 +163,14 @@
         arrived(x_ref(s, slice(None), core=1), sib_recv.at[s], "sib", s)
 
     def send_z_early():
-        remote(b_buf.at[0, 0, 0, early_rows], b_buf.at[0, 1, 0, early_rows], Z_EARLY, z_recv.at[0], to_mirror).start()
+        remote(b_buf.at[0, 0, 0, early_rows], b_buf.at[0, 1, 0, early_rows], SMALL, z_recv.at[0], to_mirror).start()
 
     def send_z_pair():
-        remote(b_ref.at[:, other_cols], b_buf.at[0, 2, 0], Z_KIND, z_recv.at[1], to_pair).start()
+        remote(b_ref.at[:, other_cols], b_buf.at[0, 2, 0], BIG, z_recv.at[1], to_pair).start()
 
     def send_z_mirror():
         z_got(2)
-        remote(b_buf.at[0, 2, 0], b_buf.at[0, 3, 0], Z_KIND, z_recv.at[2], to_mirror).start()
+        remote(b_buf.at[0, 2, 0], b_buf.at[0, 3, 0], BIG, z_recv.at[2], to_mirror).start()
 
     def late_ref(j, k, g=1, core=0):
         return b_buf.at[j, g, core, late_rows, col_half[k]]
@@ -185,12 +185,12 @@
         elif j > 0:
             x_got(0, 0)
             x_got(0, 1)
-        remote(late_ref(j, k, 0), late_ref(j, k), Z_LATE, z_late.at[j, k], to_mirror).start()
+        remote(late_ref(j, k, 0), late_ref(j, k), BIG, z_late.at[j, k], to_mirror).start()
 
     @lambda f: stepper(f, LATE)
     def late_sibling(j, k):
         late_got(j, k)
-        remote(late_ref(j, k), late_ref(j, k, core=1), SIBLING, sib_late.at[int(j in INNER), k], to_sibling).start()
+        remote(late_ref(j, k), late_ref(j, k, core=1), BIG, sib_late.at[int(j in INNER), k], to_sibling).start()
 
     def late_sibling_got(slots, k):
         arrived(late_ref(pl.ds(0, 2), k, core=1), sib_late.at[int(slots == INNER), k], "sl", slots, k)
@@ -205,9 +205,6 @@
 
     def y_whole(g, part):
         return a_buf.at[1, g, 1, first_rows] if (g, part) == (3, 1) else a_buf.at[1, g, :, part_rows[part]]
-
-    def y_kind(g, part):
-        return Y_LAST if (g, part) == (3, 1) else Y_OWN + part
 
     def y_got(g, part, n):
         arrived(y_whole(g, part), y_recv.at[g, part, n], "y", g, part, n)
@@ -223,36 +220,36 @@
         if part == 1:
             pair_got(g)
         else:
-            loaded(g)
+            loaded()
         for d in both:
             h = (d + n) % 2
-            remote(y_piece(0, g, part, h), y_piece(slot_of[d], g, part, h), y_kind(g, part), y_recv.at[g, part, n], y_peer[d]).start()
+            remote(y_piece(0, g, part, h), y_piece(slot_of[d], g, part, h), SMALL, y_recv.at[g, part, n], y_peer[d]).start()
 
     @lambda f: stepper(f, Y_STEPS)
     def forward_y(g, part):
         y_got(g, part, 0)
         for d in both:
-            remote(y_piece(slot_of[d], g, part, d), y_piece(2, g, part, d), y_kind(g, part), y_fwd.at[g, part], y_peer[d]).start()
+            remote(y_piece(slot_of[d], g, part, d), y_piece(2, g, part, d), SMALL, y_fwd.at[g, part], y_peer[d]).start()
 
     @lambda f: stepper(f, range(GROUPS))
     def send_pair(g):
-        loaded((g + 2) % 4)
+        loaded()
         if g < 3:
-            remote(a_buf.at[0, (g + 2) % 4, :, own_rows], a_buf.at[0, g, :, pair_rows], PAIR_A, pair_recv.at[g], to_pair).start()
+            remote(a_buf.at[0, (g + 2) % 4, :, own_rows], a_buf.at[0, g, :, pair_rows], SMALL, pair_recv.at[g], to_pair).start()
         else:
-            remote(a_buf.at[0, 1, 1, first_own], a_buf.at[0, 3, 1, first_rows], PAIR_LAST, pair_recv.at[3], to_pair).start()
+            remote(a_buf.at[0, 1, 1, first_own], a_buf.at[0, 3, 1, first_rows], SMALL, pair_recv.at[3], to_pair).start()
 
     @lambda f: stepper(f, (0, 1, 3, 2))
     def send_full(i):
         if i == 0:
-            loaded(1)
+            loaded()
         elif i == 2:
             far_y_got(1, 0)
         else:
             y_got(1, 0, 0)
             y_got(1, 0, 1)
-        remote(a_buf.at[i, 1, 0, own_rows], a_buf.at[i, 3, 0, pair_rows], FULL, pair_full.at[0], to_pair).start()
-        remote(a_buf.at[i, 1, 1, second_own], a_buf.at[i, 3, 1, second_rows], FULL_LAST, pair_full.at[1], to_pair).start()
+        remote(a_buf.at[i, 1, 0, own_rows], a_buf.at[i, 3, 0, pair_rows], BIG, pair_full.at[0], to_pair).start()
+        remote(a_buf.at[i, 1, 1, second_own], a_buf.at[i, 3, 1, second_rows], SMALL, pair_full.at[1], to_pair).start()
 
     def full_got():
         arrived(a_buf.at[:, 3, 0, pair_rows], pair_full.at[0], "full", 0)
@@ -260,7 +257,7 @@
 
     def ready(g, part, first, count, slots):
         if part == 0:
-            loaded(g)
+            loaded()
         else:
             pair_got(g)
         if (g, part) == (3, 1):
@@ -320,7 +317,7 @@
     def send_c(s):
         _, _, first, count = X_STEPS[s]
         at = pl.ds(pl.multiple_of(side * half + first * unit, unit), count * unit)
-        remote(stage.at[:, pl.ds(first * unit, count * unit)], out_ref.at[:, at], C_KIND, c_recv, to_pair).start()
+        remote(stage.at[:, pl.ds(first * unit, count * unit)], out_ref.at[:, at], BIG, c_recv, to_pair).start()
 
     b_load.wait()
     send_pair()
@@ -451,20 +448,8 @@
     compute()
     compute()
 
-    sent(b_buf.at[pl.ds(0, 3), pl.ds(0, 3), 0], X_KIND)
-    sent(b_buf.at[pl.ds(0, 3), 0, 0, early_rows], X_EARLY)
-    sent(a_buf.at[pl.ds(0, 3), :, :, own_rows], Y_OWN)
-    sent(a_buf.at[pl.ds(0, 3), pl.ds(0, 3), :, pair_rows], Y_PAIR)
-    sent(a_buf.at[pl.ds(0, 3), 3, 1, first_rows], Y_LAST)
-    sent(a_buf.at[0, pl.ds(0, 3), :, own_rows], PAIR_A)
-    sent(a_buf.at[0, 3, 1, first_rows], PAIR_LAST)
-    sent(a_buf.at[:, 0, 0, own_rows], FULL)
-    sent(a_buf.at[:, 3, 1, second_rows], FULL_LAST)
-    sent(b_buf.at[0, pl.ds(0, 2), 0], Z_KIND)
-    sent(b_buf.at[0, 0, 0, early_rows], Z_EARLY)
-    sent(b_buf.at[:, 0, 0, late_rows], Z_LATE)
-    sent(b_buf.at[:, :, 0], SIBLING)
-    sent(stage, C_KIND)
+    sent(b_buf, BIG)
+    sent(a_buf.at[:, :, :, pl.ds(0, rows + rows * 3 // 4)], SMALL)
     arrived(out_ref.at[:, other_cols], c_recv, "c")
 
 
@@ -483,7 +468,7 @@
                 pltpu.VMEM((4, GROUPS, 2, rows, half), jnp.bfloat16),
                 pltpu.VMEM((2 * rows, half), jnp.float32),
                 pltpu.VMEM((rows, half), jnp.bfloat16),
-                dma((GROUPS + 1,)),
+                dma((2,)),
                 dma((GROUPS, 2, 2)),
                 dma((GROUPS, 2)),
                 dma((GROUPS,)),
@@ -495,7 +480,7 @@
                 dma((len(X_STEPS),)),
                 dma((2, 2)),
                 dma(()),
-                dma((14,)),
+                dma((2,)),
             ],
             compiler_params=pltpu.CompilerParams(collective_id=0, has_side_effects=True, vmem_limit_bytes=56 * 1024 * 1024),
         )(a_blk, b_blk)

time: 72.8 us -> 72.6 us (level)
  no operation moved by 1% of the time
where the time goes in v8:
time: 72.6 us; the launch traced here: 72.5 us
  Pallas kernels  71.5 us (98%)
  local copies, waits for them, and re-layouts  0.97 us (1%)
    pallas_call x1, Pallas kernels, product(): pl.pallas_call(kernel, out_shape=pltpu.VMEM((rows, width), jnp.bfloat16),...  71.5 us

profile of v8, /device:TPU:1, one launch (start us, length us, event | category | flops | bytes accessed | tf_op | source)
XLA Modules:
  0.0 72.5 jit_solution(4123861267458666747)
XLA Ops:
  0.0 71.5 %shard_map.28 = bf16[256,2048]{1,0:T(8,128)(2,1)S(1)} custom-call(bf16[256,2048]{1,0:T(8,128)(2,1)} %a_ref.1, bf16[256,2048]{1,0:T(8,128)(2,1)} %b_ref.1), custom_call_target="tpu_custom_call" | custom-call | tf_op jit(solution)/shard_map/pallas_call | solution.py:461
  71.5 1.0 %copy.4 = bf16[256,2048]{1,0:T(8,128)(2,1)} copy(bf16[256,2048]{1,0:T(8,128)(2,1)S(1)} %shard_map.28) | data formatting | bytes 2097152

commit v9 on v8

--- a/solution.py
+++ b/solution.py
@@ -52,7 +52,7 @@
     return step
 
 
-def kernel(a_ref, b_ref, out_ref, a_buf, b_buf, acc, stage, load_sem, y_recv, y_fwd, pair_recv, pair_full, x_recv, x_fwd, z_recv, z_late, sib_recv, sib_late, c_recv, send_sem):
+def kernel(a_ref, b_ref, out_ref, a_buf, b_buf, acc, stage, load_sem, y_recv, y_fwd, pair_recv, pair_full, x_recv, x_fwd, z_recv, z_late, sib_recv, sib_late, c_recv, send_sem, ready):
     z, y, r = lax.axis_index("depth"), lax.axis_index("col"), lax.axis_index("row")
     x, c = r // 2, r % 2
     rows, width = a_ref.shape
@@ -99,10 +99,35 @@
             start = pl.multiple_of((c + cc - 2 * c * cc) * half + z_of[g] * rows, rows)
             pltpu.make_async_copy(a_ref.at[:, pl.ds(start, rows)], a_buf.at[0, g, cc, own_rows], load_sem.at[0]).start()
 
+    MIRROR = 5
+    lower = ((y + 1) % 4 < y, (y + 3) % 4 < y, (x + 1) % 4 < x, (x + 3) % 4 < x, pair < z, mirror < z, c == 0)
+    seen_there_as = (1, 0, 3, 2, 4, MIRROR, 6)
     barrier = pltpu.get_barrier_semaphore()
-    for where in peers:
-        pl.semaphore_signal(barrier, inc=1, device_id=where, device_id_type=MESH)
-    pl.semaphore_wait(barrier, len(peers))
+    for is_lower, where in zip(lower, peers):
+
+        @pl.when(jnp.logical_not(is_lower))
+        def _(where=where):
+            pl.semaphore_signal(barrier, inc=1, device_id=where, device_id_type=MESH)
+
+    awaited = sum(is_lower.astype(jnp.int32) for is_lower in lower)
+
+    @pl.when(awaited > 0)
+    def _():
+        pl.semaphore_wait(barrier, awaited)
+
+    for is_lower, where, index in zip(lower, peers, seen_there_as):
+
+        @pl.when(is_lower)
+        def _(where=where, index=index):
+            pl.semaphore_signal(ready.at[index], inc=1, device_id=where, device_id_type=MESH)
+
+    def met(peer):
+        if ("met", peer) not in waited:
+            waited.add(("met", peer))
+
+            @pl.when(jnp.logical_not(lower[peer]))
+            def _():
+                pl.semaphore_wait(ready.at[peer], 1)
 
     def loaded():
         arrived(a_buf.at[0, :, :, own_rows], load_sem.at[0], "load")
@@ -163,6 +188,7 @@
         arrived(x_ref(s, slice(None), core=1), sib_recv.at[s], "sib", s)
 
     def send_z_early():
+        met(MIRROR)
         remote(b_buf.at[0, 0, 0, early_rows], b_buf.at[0, 1, 0, early_rows], SMALL, z_recv.at[0], to_mirror).start()
 
     def send_z_pair():
@@ -185,6 +211,7 @@
         elif j > 0:
             x_got(0, 0)
             x_got(0, 1)
+        met(MIRROR)
         remote(late_ref(j, k, 0), late_ref(j, k), BIG, z_late.at[j, k], to_mirror).start()
 
     @lambda f: stepper(f, LATE)
@@ -255,7 +282,7 @@
         arrived(a_buf.at[:, 3, 0, pair_rows], pair_full.at[0], "full", 0)
         arrived(a_buf.at[:, 3, 1, second_rows], pair_full.at[1], "full", 1)
 
-    def ready(g, part, first, count, slots):
+    def inputs_got(g, part, first, count, slots):
         if part == 0:
             loaded()
         else:
@@ -282,7 +309,7 @@
 
     @lambda f: stepper(f, PRODUCTS)
     def compute(g, part, first, count, slots):
-        ready(g, part, first, count, slots)
+        inputs_got(g, part, first, count, slots)
         by_a = slots in (NEAR, FAR)
         last = g == 3 and slots != NEAR
         add = g > 0
@@ -320,18 +347,20 @@
         remote(stage.at[:, pl.ds(first * unit, count * unit)], out_ref.at[:, at], BIG, c_recv, to_pair).start()
 
     b_load.wait()
+    for peer in (6, 2, 0, 4, 3, 1):
+        met(peer)
     send_pair()
     send_y()
     send_x()
     send_x()
     send_z_pair()
+    send_pair()
+    send_y()
+    send_y()
+    send_y()
+    send_pair()
     send_z_early()
-    send_pair()
-    send_y()
-    send_y()
-    send_late()
-    send_y()
-    send_pair()
+    send_late()
     send_x()
     send_x()
     forward_x()
@@ -481,6 +510,7 @@
                 dma((2, 2)),
                 dma(()),
                 dma((2,)),
+                pltpu.SemaphoreType.REGULAR((7,)),
             ],
             compiler_params=pltpu.CompilerParams(collective_id=0, has_side_effects=True, vmem_limit_bytes=56 * 1024 * 1024),
         )(a_blk, b_blk)

time: 72.6 us -> 73.5 us (1.012)
  Pallas kernels: 71.5 us -> 72.4 us
    pallas_call x1, Pallas kernels: 71.5 us -> 72.4 us  [product(): pl.pallas_call(kernel, out_shape=pltpu.VMEM((rows, width), jnp.bfloat16),...]
where the time goes in v9:
time: 73.5 us; the launch traced here: 73.4 us
  Pallas kernels  72.4 us (99%)
  local copies, waits for them, and re-layouts  0.97 us (1%)
    pallas_call x1, Pallas kernels, product(): pl.pallas_call(kernel, out_shape=pltpu.VMEM((rows, width), jnp.bfloat16),...  72.4 us

profile of v9, /device:TPU:1, one launch (start us, length us, event | category | flops | bytes accessed | tf_op | source)
XLA Modules:
  0.0 73.4 jit_solution(6018803208944866833)
XLA Ops:
  0.0 72.4 %shard_map.28 = bf16[256,2048]{1,0:T(8,128)(2,1)S(1)} custom-call(bf16[256,2048]{1,0:T(8,128)(2,1)} %a_ref.1, bf16[256,2048]{1,0:T(8,128)(2,1)} %b_ref.1), custom_call_target="tpu_custom_call" | custom-call | tf_op jit(solution)/shard_map/pallas_call | solution.py:490
  72.4 1.0 %copy.4 = bf16[256,2048]{1,0:T(8,128)(2,1)} copy(bf16[256,2048]{1,0:T(8,128)(2,1)S(1)} %shard_map.28) | data formatting | bytes 2097152

commit v10 on v9

--- a/solution.py
+++ b/solution.py
@@ -15,28 +15,28 @@
 Y_STEPS = ((0, 0), (1, 0), (0, 1), (1, 1), (2, 1), (3, 1), (2, 0), (3, 0))
 LATE = ((0, 0), (0, 1), (3, 0), (3, 1), (1, 0), (2, 0), (1, 1), (2, 1))
 PRODUCTS = (
-    (0, 0, 4, 4, ALL),
     (0, 1, 4, 4, ALL),
     (0, 0, 0, 4, ALL),
     (0, 1, 0, 4, ALL),
     (1, 0, 0, 4, OUTER),
-    (1, 0, 4, 4, OUTER),
+    (1, 1, 0, 4, OUTER),
     (1, 1, 4, 4, OUTER),
+    (1, 1, 0, 4, INNER),
     (2, 1, 0, 4, ALL),
-    (1, 1, 0, 4, OUTER),
-    (1, 1, 0, 4, INNER),
-    (1, 0, 0, 4, INNER),
     (3, 1, 0, 2, ALL),
     (2, 1, 4, 4, ALL),
     (3, 1, 2, 2, ALL),
+    (1, 0, 0, 4, INNER),
     (1, 1, 4, 4, INNER),
     (3, 1, 4, 2, ALL),
+    (0, 0, 4, 4, ALL),
     (1, 0, 4, 4, INNER),
+    (1, 0, 4, 4, OUTER),
     (3, 1, 6, 1, ALL),
     (2, 0, 4, 4, ALL),
     (3, 1, 7, 1, ALL),
+    (3, 0, 0, 8, NEAR),
     (2, 0, 0, 4, ALL),
-    (3, 0, 0, 8, NEAR),
     (3, 0, 0, 8, FAR),
 )
 BIG, SMALL = range(2)
@@ -349,127 +349,127 @@
     b_load.wait()
     for peer in (6, 2, 0, 4, 3, 1):
         met(peer)
+    send_x()
+    send_y()
     send_pair()
-    send_y()
-    send_x()
-    send_x()
     send_z_pair()
+    send_x()
     send_pair()
     send_y()
     send_y()
     send_y()
     send_pair()
+    send_late()
     send_z_early()
     send_late()
-    send_x()
-    send_x()
-    forward_x()
-    send_late()
-    forward_y()
-    sib_own()
-    send_y()
-    late_sibling()
-    send_y()
-    sib_near()
-    send_late()
-    forward_y()
-    send_late()
-    sib_near()
-    sib_own()
+    forward_y()
+    send_y()
+    send_y()
+    forward_x()
+    forward_y()
+    send_late()
+    send_x()
+    sib_own()
+    late_sibling()
+    send_pair()
+    send_x()
+    send_late()
+    sib_far()
+    send_x()
+    send_full()
+    forward_y()
+    late_sibling()
     send_z_mirror()
-    send_x()
-    forward_y()
-    send_pair()
-    send_y()
-    send_late()
-    sib_far()
-    send_x()
-    send_y()
+    sib_near()
+    forward_x()
     send_full()
-    forward_x()
-    forward_x()
+    send_x()
+    late_sibling()
+    send_y()
+    send_y()
     send_full()
-    late_sibling()
-    send_y()
-    send_y()
-    late_sibling()
-    send_y()
-    sib_own()
-    send_late()
-    compute()
+    sib_near()
+    send_late()
+    forward_y()
+    compute()
+    sib_own()
+    sib_far()
+    forward_x()
+    send_y()
+    send_y()
+    sib_own()
+    send_late()
+    send_y()
+    send_late()
+    sib_near()
+    sib_own()
+    send_x()
     send_full()
-    compute()
-    compute()
-    sib_own()
-    forward_y()
-    late_sibling()
-    sib_own()
-    send_x()
-    send_x()
-    send_x()
-    compute()
-    send_late()
-    forward_y()
-    send_x()
-    sib_far()
-    sib_far()
-    send_y()
-    send_y()
-    sib_near()
-    send_late()
-    compute()
-    forward_x()
-    send_x()
-    send_full()
-    late_sibling()
-    sib_near()
-    compute()
-    compute()
-    forward_y()
-    forward_x()
-    send_y()
-    late_sibling()
-    send_y()
-    compute()
-    compute()
-    sib_own()
-    send_x()
-    compute()
-    send_x()
-    sib_far()
-    sib_near()
-    forward_y()
-    forward_x()
-    compute()
-    send_x()
-    send_x()
-    compute()
+    send_x()
+    compute()
+    send_x()
+    send_x()
+    late_sibling()
+    send_y()
+    forward_y()
+    sib_own()
+    send_y()
+    sib_own()
+    compute()
+    forward_y()
+    forward_x()
+    sib_own()
+    sib_far()
+    late_sibling()
+    send_y()
+    send_x()
+    compute()
+    send_late()
+    compute()
+    late_sibling()
+    send_y()
+    forward_x()
+    send_x()
+    send_x()
+    compute()
+    sib_own()
+    sib_near()
+    compute()
+    sib_far()
+    send_x()
+    compute()
+    forward_x()
+    compute()
+    send_x()
     send_c()
-    sib_far()
-    late_sibling()
-    compute()
-    compute()
-    late_sibling()
-    sib_near()
-    forward_x()
+    sib_near()
+    send_x()
+    late_sibling()
+    forward_y()
+    sib_far()
+    compute()
+    compute()
+    send_y()
     send_c()
-    sib_far()
-    send_y()
-    send_x()
-    compute()
-    forward_x()
-    sib_own()
-    compute()
-    sib_near()
+    forward_x()
+    sib_near()
+    late_sibling()
+    sib_far()
+    compute()
+    forward_x()
+    compute()
+    compute()
     send_c()
-    sib_own()
-    forward_y()
-    compute()
-    sib_far()
-    sib_near()
-    compute()
+    sib_near()
+    forward_y()
+    compute()
+    sib_far()
+    compute()
+    sib_near()
+    compute()
+    compute()
+    sib_far()
     send_c()
-    sib_far()
     compute()
     compute()
     send_c()

time: 73.5 us -> 72.3 us (0.984)
  Pallas kernels: 72.4 us -> 71.2 us
    pallas_call x1, Pallas kernels: 72.4 us -> 71.2 us  [product(): pl.pallas_call(kernel, out_shape=pltpu.VMEM((rows, width), jnp.bfloat16),...]
where the time goes in v10:
time: 72.3 us; the launch traced here: 72.2 us
  Pallas kernels  71.2 us (98%)
  local copies, waits for them, and re-layouts  0.97 us (1%)
    pallas_call x1, Pallas kernels, product(): pl.pallas_call(kernel, out_shape=pltpu.VMEM((rows, width), jnp.bfloat16),...  71.2 us

profile of v10, /device:TPU:1, one launch (start us, length us, event | category | flops | bytes accessed | tf_op | source)
XLA Modules:
  0.0 72.2 jit_solution(3321697674618406871)
XLA Ops:
  0.0 71.2 %shard_map.28 = bf16[256,2048]{1,0:T(8,128)(2,1)S(1)} custom-call(bf16[256,2048]{1,0:T(8,128)(2,1)} %a_ref.1, bf16[256,2048]{1,0:T(8,128)(2,1)} %b_ref.1), custom_call_target="tpu_custom_call" | custom-call | tf_op jit(solution)/shard_map/pallas_call | solution.py:490
  71.2 1.0 %copy.4 = bf16[256,2048]{1,0:T(8,128)(2,1)} copy(bf16[256,2048]{1,0:T(8,128)(2,1)S(1)} %shard_map.28) | data formatting | bytes 2097152

commit v11 on v10

--- a/solution.py
+++ b/solution.py
@@ -52,7 +52,7 @@
     return step
 
 
-def kernel(a_ref, b_ref, out_ref, a_buf, b_buf, acc, stage, load_sem, y_recv, y_fwd, pair_recv, pair_full, x_recv, x_fwd, z_recv, z_late, sib_recv, sib_late, c_recv, send_sem, ready):
+def kernel(a_ref, b_ref, out_ref, a_buf, b_buf, acc, stage, load_sem, y_recv, y_fwd, pair_recv, pair_full, x_recv, x_fwd, z_recv, z_late, sib_recv, sib_late, c_recv, send_sem):
     z, y, r = lax.axis_index("depth"), lax.axis_index("col"), lax.axis_index("row")
     x, c = r // 2, r % 2
     rows, width = a_ref.shape
@@ -99,35 +99,10 @@
             start = pl.multiple_of((c + cc - 2 * c * cc) * half + z_of[g] * rows, rows)
             pltpu.make_async_copy(a_ref.at[:, pl.ds(start, rows)], a_buf.at[0, g, cc, own_rows], load_sem.at[0]).start()
 
-    MIRROR = 5
-    lower = ((y + 1) % 4 < y, (y + 3) % 4 < y, (x + 1) % 4 < x, (x + 3) % 4 < x, pair < z, mirror < z, c == 0)
-    seen_there_as = (1, 0, 3, 2, 4, MIRROR, 6)
     barrier = pltpu.get_barrier_semaphore()
-    for is_lower, where in zip(lower, peers):
-
-        @pl.when(jnp.logical_not(is_lower))
-        def _(where=where):
-            pl.semaphore_signal(barrier, inc=1, device_id=where, device_id_type=MESH)
-
-    awaited = sum(is_lower.astype(jnp.int32) for is_lower in lower)
-
-    @pl.when(awaited > 0)
-    def _():
-        pl.semaphore_wait(barrier, awaited)
-
-    for is_lower, where, index in zip(lower, peers, seen_there_as):
-
-        @pl.when(is_lower)
-        def _(where=where, index=index):
-            pl.semaphore_signal(ready.at[index], inc=1, device_id=where, device_id_type=MESH)
-
-    def met(peer):
-        if ("met", peer) not in waited:
-            waited.add(("met", peer))
-
-            @pl.when(jnp.logical_not(lower[peer]))
-            def _():
-                pl.semaphore_wait(ready.at[peer], 1)
+    for where in peers:
+        pl.semaphore_signal(barrier, inc=1, device_id=where, device_id_type=MESH)
+    pl.semaphore_wait(barrier, len(peers))
 
     def loaded():
         arrived(a_buf.at[0, :, :, own_rows], load_sem.at[0], "load")
@@ -188,7 +163,6 @@
         arrived(x_ref(s, slice(None), core=1), sib_recv.at[s], "sib", s)
 
     def send_z_early():
-        met(MIRROR)
         remote(b_buf.at[0, 0, 0, early_rows], b_buf.at[0, 1, 0, early_rows], SMALL, z_recv.at[0], to_mirror).start()
 
     def send_z_pair():
@@ -211,7 +185,6 @@
         elif j > 0:
             x_got(0, 0)
             x_got(0, 1)
-        met(MIRROR)
         remote(late_ref(j, k, 0), late_ref(j, k), BIG, z_late.at[j, k], to_mirror).start()
 
     @lambda f: stepper(f, LATE)
@@ -282,7 +255,7 @@
         arrived(a_buf.at[:, 3, 0, pair_rows], pair_full.at[0], "full", 0)
         arrived(a_buf.at[:, 3, 1, second_rows], pair_full.at[1], "full", 1)
 
-    def inputs_got(g, part, first, count, slots):
+    def ready(g, part, first, count, slots):
         if part == 0:
             loaded()
         else:
@@ -309,7 +282,7 @@
 
     @lambda f: stepper(f, PRODUCTS)
     def compute(g, part, first, count, slots):
-        inputs_got(g, part, first, count, slots)
+        ready(g, part, first, count, slots)
         by_a = slots in (NEAR, FAR)
         last = g == 3 and slots != NEAR
         add = g > 0
@@ -347,21 +320,19 @@
         remote(stage.at[:, pl.ds(first * unit, count * unit)], out_ref.at[:, at], BIG, c_recv, to_pair).start()
 
     b_load.wait()
-    for peer in (6, 2, 0, 4, 3, 1):
-        met(peer)
     send_x()
     send_y()
     send_pair()
+    send_late()
     send_z_pair()
     send_x()
     send_pair()
+    send_z_early()
+    send_late()
     send_y()
     send_y()
     send_y()
     send_pair()
-    send_late()
-    send_z_early()
-    send_late()
     forward_y()
     send_y()
     send_y()
@@ -510,7 +481,6 @@
                 dma((2, 2)),
                 dma(()),
                 dma((2,)),
-                pltpu.SemaphoreType.REGULAR((7,)),
             ],
             compiler_params=pltpu.CompilerParams(collective_id=0, has_side_effects=True, vmem_limit_bytes=56 * 1024 * 1024),
         )(a_blk, b_blk)

time: 72.3 us -> 71.8 us (level)
  no operation moved by 1% of the time
where the time goes in v11:
time: 71.8 us; the launch traced here: 71.7 us
  Pallas kernels  70.7 us (98%)
  local copies, waits for them, and re-layouts  0.97 us (1%)
    pallas_call x1, Pallas kernels, product(): pl.pallas_call(kernel, out_shape=pltpu.VMEM((rows, width), jnp.bfloat16),...  70.7 us

profile of v11, /device:TPU:1, one launch (start us, length us, event | category | flops | bytes accessed | tf_op | source)
XLA Modules:
  0.0 71.7 jit_solution(2437111579791480701)
XLA Ops:
  0.0 70.7 %shard_map.28 = bf16[256,2048]{1,0:T(8,128)(2,1)S(1)} custom-call(bf16[256,2048]{1,0:T(8,128)(2,1)} %a_ref.1, bf16[256,2048]{1,0:T(8,128)(2,1)} %b_ref.1), custom_call_target="tpu_custom_call" | custom-call | tf_op jit(solution)/shard_map/pallas_call | solution.py:461
  70.7 1.0 %copy.4 = bf16[256,2048]{1,0:T(8,128)(2,1)} copy(bf16[256,2048]{1,0:T(8,128)(2,1)S(1)} %shard_map.28) | data formatting | bytes 2097152

commit v12 on v11

--- a/solution.py
+++ b/solution.py
@@ -15,23 +15,23 @@
 Y_STEPS = ((0, 0), (1, 0), (0, 1), (1, 1), (2, 1), (3, 1), (2, 0), (3, 0))
 LATE = ((0, 0), (0, 1), (3, 0), (3, 1), (1, 0), (2, 0), (1, 1), (2, 1))
 PRODUCTS = (
-    (0, 1, 4, 4, ALL),
     (0, 0, 0, 4, ALL),
     (0, 1, 0, 4, ALL),
-    (1, 0, 0, 4, OUTER),
+    (0, 1, 4, 4, ALL),
+    (0, 0, 4, 4, ALL),
     (1, 1, 0, 4, OUTER),
     (1, 1, 4, 4, OUTER),
+    (2, 1, 0, 4, ALL),
     (1, 1, 0, 4, INNER),
-    (2, 1, 0, 4, ALL),
+    (1, 0, 4, 4, OUTER),
     (3, 1, 0, 2, ALL),
+    (1, 0, 0, 4, OUTER),
     (2, 1, 4, 4, ALL),
     (3, 1, 2, 2, ALL),
     (1, 0, 0, 4, INNER),
     (1, 1, 4, 4, INNER),
     (3, 1, 4, 2, ALL),
-    (0, 0, 4, 4, ALL),
     (1, 0, 4, 4, INNER),
-    (1, 0, 4, 4, OUTER),
     (3, 1, 6, 1, ALL),
     (2, 0, 4, 4, ALL),
     (3, 1, 7, 1, ALL),
@@ -320,127 +320,127 @@
         remote(stage.at[:, pl.ds(first * unit, count * unit)], out_ref.at[:, at], BIG, c_recv, to_pair).start()
 
     b_load.wait()
-    send_x()
-    send_y()
     send_pair()
-    send_late()
+    send_x()
+    send_y()
+    send_y()
     send_z_pair()
     send_x()
+    send_z_early()
+    send_y()
+    send_late()
+    send_late()
+    send_x()
     send_pair()
-    send_z_early()
-    send_late()
-    send_y()
-    send_y()
-    send_y()
+    send_y()
+    send_x()
+    send_y()
+    forward_x()
     send_pair()
-    forward_y()
-    send_y()
-    send_y()
-    forward_x()
-    forward_y()
-    send_late()
-    send_x()
-    sib_own()
-    late_sibling()
+    send_late()
+    sib_own()
+    send_full()
+    send_y()
+    send_late()
+    forward_y()
+    late_sibling()
+    send_x()
+    forward_y()
+    sib_near()
+    forward_y()
+    send_z_mirror()
+    send_x()
+    sib_far()
     send_pair()
-    send_x()
-    send_late()
-    sib_far()
-    send_x()
+    forward_x()
+    send_y()
+    send_late()
+    send_late()
+    sib_own()
     send_full()
-    forward_y()
-    late_sibling()
-    send_z_mirror()
-    sib_near()
-    forward_x()
+    compute()
+    send_y()
+    sib_near()
+    late_sibling()
+    forward_y()
+    sib_own()
+    forward_x()
+    compute()
+    compute()
+    send_late()
+    send_y()
+    send_y()
+    compute()
+    send_x()
     send_full()
-    send_x()
-    late_sibling()
-    send_y()
+    sib_far()
+    sib_own()
+    send_late()
+    send_y()
+    late_sibling()
+    send_x()
+    sib_far()
+    forward_y()
+    sib_near()
+    send_x()
+    send_y()
+    late_sibling()
+    forward_x()
+    send_x()
+    send_x()
+    late_sibling()
     send_y()
     send_full()
-    sib_near()
-    send_late()
-    forward_y()
-    compute()
-    sib_own()
-    sib_far()
-    forward_x()
-    send_y()
-    send_y()
-    sib_own()
-    send_late()
-    send_y()
-    send_late()
-    sib_near()
-    sib_own()
-    send_x()
-    send_full()
-    send_x()
-    compute()
-    send_x()
-    send_x()
-    late_sibling()
-    send_y()
-    forward_y()
-    sib_own()
-    send_y()
-    sib_own()
-    compute()
-    forward_y()
-    forward_x()
-    sib_own()
-    sib_far()
-    late_sibling()
-    send_y()
-    send_x()
-    compute()
-    send_late()
-    compute()
-    late_sibling()
-    send_y()
-    forward_x()
-    send_x()
-    send_x()
-    compute()
-    sib_own()
-    sib_near()
-    compute()
-    sib_far()
-    send_x()
-    compute()
-    forward_x()
-    compute()
-    send_x()
+    compute()
+    sib_near()
+    forward_y()
+    compute()
+    forward_x()
+    send_y()
+    sib_far()
+    late_sibling()
+    send_x()
+    compute()
+    compute()
+    send_x()
+    send_y()
+    compute()
+    forward_x()
+    sib_near()
+    send_x()
+    send_x()
+    sib_own()
+    compute()
     send_c()
-    sib_near()
-    send_x()
-    late_sibling()
-    forward_y()
-    sib_far()
-    compute()
-    compute()
-    send_y()
+    compute()
+    sib_far()
+    forward_y()
+    compute()
+    sib_near()
+    forward_x()
+    sib_own()
+    compute()
+    late_sibling()
+    sib_own()
     send_c()
-    forward_x()
-    sib_near()
-    late_sibling()
-    sib_far()
-    compute()
+    send_y()
+    send_x()
+    late_sibling()
+    compute()
+    sib_far()
+    sib_own()
     forward_x()
     compute()
     compute()
     send_c()
     sib_near()
-    forward_y()
-    compute()
-    sib_far()
-    compute()
-    sib_near()
-    compute()
-    compute()
-    sib_far()
+    sib_far()
+    sib_near()
+    compute()
+    forward_y()
+    compute()
     send_c()
+    sib_far()
     compute()
     compute()
     send_c()

time: 71.8 us -> 72.4 us (level)
  no operation moved by 1% of the time
where the time goes in v12:
time: 72.4 us; the launch traced here: 72.3 us
  Pallas kernels  71.3 us (98%)
  local copies, waits for them, and re-layouts  0.97 us (1%)
    pallas_call x1, Pallas kernels, product(): pl.pallas_call(kernel, out_shape=pltpu.VMEM((rows, width), jnp.bfloat16),...  71.3 us

profile of v12, /device:TPU:1, one launch (start us, length us, event | category | flops | bytes accessed | tf_op | source)
XLA Modules:
  0.0 72.3 jit_solution(18013438267631341586)
XLA Ops:
  0.0 71.3 %shard_map.28 = bf16[256,2048]{1,0:T(8,128)(2,1)S(1)} custom-call(bf16[256,2048]{1,0:T(8,128)(2,1)} %a_ref.1, bf16[256,2048]{1,0:T(8,128)(2,1)} %b_ref.1), custom_call_target="tpu_custom_call" | custom-call | tf_op jit(solution)/shard_map/pallas_call | solution.py:461
  71.3 1.0 %copy.4 = bf16[256,2048]{1,0:T(8,128)(2,1)} copy(bf16[256,2048]{1,0:T(8,128)(2,1)S(1)} %shard_map.28) | data formatting | bytes 2097152

commit v13 on v8

--- a/solution.py
+++ b/solution.py
@@ -15,19 +15,19 @@
 Y_STEPS = ((0, 0), (1, 0), (0, 1), (1, 1), (2, 1), (3, 1), (2, 0), (3, 0))
 LATE = ((0, 0), (0, 1), (3, 0), (3, 1), (1, 0), (2, 0), (1, 1), (2, 1))
 PRODUCTS = (
+    (0, 1, 0, 4, ALL),
     (0, 0, 4, 4, ALL),
     (0, 1, 4, 4, ALL),
+    (1, 1, 0, 4, OUTER),
+    (1, 1, 4, 4, OUTER),
     (0, 0, 0, 4, ALL),
-    (0, 1, 0, 4, ALL),
+    (1, 0, 4, 4, OUTER),
+    (2, 1, 4, 4, ALL),
+    (2, 1, 0, 4, ALL),
+    (1, 1, 0, 4, INNER),
+    (3, 1, 0, 2, ALL),
+    (1, 0, 0, 4, INNER),
     (1, 0, 0, 4, OUTER),
-    (1, 0, 4, 4, OUTER),
-    (1, 1, 4, 4, OUTER),
-    (2, 1, 0, 4, ALL),
-    (1, 1, 0, 4, OUTER),
-    (1, 1, 0, 4, INNER),
-    (1, 0, 0, 4, INNER),
-    (3, 1, 0, 2, ALL),
-    (2, 1, 4, 4, ALL),
     (3, 1, 2, 2, ALL),
     (1, 1, 4, 4, INNER),
     (3, 1, 4, 2, ALL),
@@ -320,123 +320,123 @@
         remote(stage.at[:, pl.ds(first * unit, count * unit)], out_ref.at[:, at], BIG, c_recv, to_pair).start()
 
     b_load.wait()
+    send_y()
+    send_y()
     send_pair()
-    send_y()
-    send_x()
-    send_x()
+    send_x()
+    send_z_early()
+    sib_own()
+    send_x()
+    send_y()
     send_z_pair()
-    send_z_early()
+    send_y()
+    send_x()
+    sib_own()
     send_pair()
-    send_y()
-    send_y()
-    send_late()
-    send_y()
+    send_late()
+    send_y()
+    send_late()
+    forward_x()
     send_pair()
-    send_x()
-    send_x()
-    forward_x()
-    send_late()
-    forward_y()
-    sib_own()
-    send_y()
-    late_sibling()
-    send_y()
-    sib_near()
-    send_late()
-    forward_y()
-    send_late()
-    sib_near()
-    sib_own()
+    send_y()
+    late_sibling()
+    forward_y()
+    send_pair()
+    send_late()
+    forward_y()
+    sib_near()
+    late_sibling()
+    forward_x()
+    send_full()
+    send_late()
+    send_x()
     send_z_mirror()
-    send_x()
-    forward_y()
-    send_pair()
-    send_y()
-    send_late()
-    sib_far()
-    send_x()
+    forward_y()
+    send_x()
+    sib_near()
+    send_late()
     send_y()
     send_full()
-    forward_x()
-    forward_x()
+    send_x()
+    send_late()
+    late_sibling()
+    send_y()
+    send_y()
+    sib_far()
+    sib_own()
+    forward_y()
+    send_y()
+    sib_far()
+    send_y()
+    send_y()
+    forward_x()
+    compute()
+    compute()
+    send_late()
+    sib_near()
     send_full()
-    late_sibling()
-    send_y()
-    send_y()
-    late_sibling()
-    send_y()
-    sib_own()
-    send_late()
-    compute()
+    send_x()
+    send_x()
+    compute()
+    late_sibling()
+    send_x()
+    forward_y()
+    compute()
+    send_x()
     send_full()
-    compute()
-    compute()
-    sib_own()
-    forward_y()
-    late_sibling()
-    sib_own()
-    send_x()
-    send_x()
-    send_x()
-    compute()
-    send_late()
-    forward_y()
-    send_x()
-    sib_far()
-    sib_far()
-    send_y()
-    send_y()
-    sib_near()
-    send_late()
-    compute()
-    forward_x()
-    send_x()
-    send_full()
-    late_sibling()
-    sib_near()
-    compute()
-    compute()
-    forward_y()
-    forward_x()
-    send_y()
-    late_sibling()
-    send_y()
-    compute()
-    compute()
-    sib_own()
-    send_x()
-    compute()
-    send_x()
-    sib_far()
-    sib_near()
-    forward_y()
-    forward_x()
-    compute()
-    send_x()
-    send_x()
+    sib_own()
+    compute()
+    compute()
+    forward_x()
+    send_y()
+    send_x()
+    compute()
+    forward_y()
+    late_sibling()
+    sib_far()
+    forward_x()
+    send_y()
+    send_x()
+    send_y()
+    sib_near()
+    send_late()
+    compute()
+    sib_own()
+    send_x()
+    late_sibling()
+    sib_far()
+    sib_own()
+    compute()
+    sib_own()
+    compute()
+    forward_x()
     compute()
     send_c()
     sib_far()
-    late_sibling()
-    compute()
-    compute()
-    late_sibling()
-    sib_near()
-    forward_x()
+    send_x()
+    send_x()
+    sib_near()
+    compute()
+    forward_y()
+    compute()
+    late_sibling()
+    sib_near()
+    forward_x()
+    compute()
     send_c()
-    sib_far()
-    send_y()
-    send_x()
-    compute()
-    forward_x()
-    sib_own()
-    compute()
-    sib_near()
+    late_sibling()
+    send_x()
+    send_y()
+    sib_far()
+    sib_near()
+    compute()
+    forward_x()
+    compute()
     send_c()
-    sib_own()
-    forward_y()
-    compute()
-    sib_far()
+    sib_far()
+    forward_y()
+    sib_own()
+    compute()
     sib_near()
     compute()
     send_c()

time: 72.6 us -> 71.6 us (0.986)
  Pallas kernels: 71.5 us -> 70.5 us
    pallas_call x1, Pallas kernels: 71.5 us -> 70.5 us  [product(): pl.pallas_call(kernel, out_shape=pltpu.VMEM((rows, width), jnp.bfloat16),...]
where the time goes in v13:
time: 71.6 us; the launch traced here: 71.5 us
  Pallas kernels  70.5 us (98%)
  local copies, waits for them, and re-layouts  0.97 us (1%)
    pallas_call x1, Pallas kernels, product(): pl.pallas_call(kernel, out_shape=pltpu.VMEM((rows, width), jnp.bfloat16),...  70.5 us

profile of v13, /device:TPU:1, one launch (start us, length us, event | category | flops | bytes accessed | tf_op | source)
XLA Modules:
  0.0 71.5 jit_solution(8256504466140140243)
XLA Ops:
  0.0 70.5 %shard_map.28 = bf16[256,2048]{1,0:T(8,128)(2,1)S(1)} custom-call(bf16[256,2048]{1,0:T(8,128)(2,1)} %a_ref.1, bf16[256,2048]{1,0:T(8,128)(2,1)} %b_ref.1), custom_call_target="tpu_custom_call" | custom-call | tf_op jit(solution)/shard_map/pallas_call | solution.py:461
  70.5 1.0 %copy.4 = bf16[256,2048]{1,0:T(8,128)(2,1)} copy(bf16[256,2048]{1,0:T(8,128)(2,1)S(1)} %shard_map.28) | data formatting | bytes 2097152

commit v14 on v11

--- a/solution.py
+++ b/solution.py
@@ -15,28 +15,28 @@
 Y_STEPS = ((0, 0), (1, 0), (0, 1), (1, 1), (2, 1), (3, 1), (2, 0), (3, 0))
 LATE = ((0, 0), (0, 1), (3, 0), (3, 1), (1, 0), (2, 0), (1, 1), (2, 1))
 PRODUCTS = (
+    (0, 0, 4, 4, ALL),
     (0, 1, 4, 4, ALL),
     (0, 0, 0, 4, ALL),
+    (1, 1, 4, 4, OUTER),
+    (1, 0, 0, 4, OUTER),
+    (1, 0, 4, 4, OUTER),
     (0, 1, 0, 4, ALL),
-    (1, 0, 0, 4, OUTER),
     (1, 1, 0, 4, OUTER),
-    (1, 1, 4, 4, OUTER),
+    (2, 1, 0, 4, ALL),
     (1, 1, 0, 4, INNER),
-    (2, 1, 0, 4, ALL),
     (3, 1, 0, 2, ALL),
     (2, 1, 4, 4, ALL),
     (3, 1, 2, 2, ALL),
     (1, 0, 0, 4, INNER),
     (1, 1, 4, 4, INNER),
     (3, 1, 4, 2, ALL),
-    (0, 0, 4, 4, ALL),
     (1, 0, 4, 4, INNER),
-    (1, 0, 4, 4, OUTER),
     (3, 1, 6, 1, ALL),
+    (2, 0, 0, 4, ALL),
+    (3, 1, 7, 1, ALL),
     (2, 0, 4, 4, ALL),
-    (3, 1, 7, 1, ALL),
     (3, 0, 0, 8, NEAR),
-    (2, 0, 0, 4, ALL),
     (3, 0, 0, 8, FAR),
 )
 BIG, SMALL = range(2)
@@ -320,122 +320,122 @@
         remote(stage.at[:, pl.ds(first * unit, count * unit)], out_ref.at[:, at], BIG, c_recv, to_pair).start()
 
     b_load.wait()
-    send_x()
-    send_y()
+    send_y()
+    send_x()
+    send_x()
+    send_y()
+    send_y()
+    send_z_early()
     send_pair()
-    send_late()
     send_z_pair()
-    send_x()
+    sib_own()
+    send_late()
+    send_y()
+    send_y()
     send_pair()
-    send_z_early()
-    send_late()
-    send_y()
-    send_y()
-    send_y()
+    send_y()
+    send_x()
+    send_late()
     send_pair()
-    forward_y()
-    send_y()
-    send_y()
-    forward_x()
-    forward_y()
-    send_late()
-    send_x()
-    sib_own()
-    late_sibling()
+    sib_own()
+    forward_x()
+    forward_y()
+    send_late()
+    send_late()
+    forward_x()
+    forward_y()
+    forward_y()
     send_pair()
     send_x()
-    send_late()
-    sib_far()
-    send_x()
+    send_z_mirror()
+    send_x()
+    late_sibling()
+    send_y()
+    send_y()
+    sib_far()
+    sib_near()
+    late_sibling()
     send_full()
-    forward_y()
-    late_sibling()
-    send_z_mirror()
-    sib_near()
+    send_x()
+    send_y()
     forward_x()
     send_full()
-    send_x()
-    late_sibling()
-    send_y()
-    send_y()
+    forward_y()
+    sib_near()
+    send_late()
+    compute()
+    send_y()
+    send_x()
+    send_late()
+    send_y()
+    late_sibling()
+    send_x()
+    compute()
+    sib_near()
     send_full()
-    sib_near()
-    send_late()
-    forward_y()
-    compute()
-    sib_own()
-    sib_far()
-    forward_x()
-    send_y()
-    send_y()
-    sib_own()
-    send_late()
-    send_y()
-    send_late()
-    sib_near()
-    sib_own()
-    send_x()
     send_full()
-    send_x()
-    compute()
-    send_x()
-    send_x()
-    late_sibling()
-    send_y()
-    forward_y()
-    sib_own()
-    send_y()
-    sib_own()
-    compute()
-    forward_y()
-    forward_x()
-    sib_own()
-    sib_far()
-    late_sibling()
-    send_y()
-    send_x()
-    compute()
-    send_late()
-    compute()
-    late_sibling()
-    send_y()
-    forward_x()
-    send_x()
-    send_x()
-    compute()
-    sib_own()
-    sib_near()
-    compute()
-    sib_far()
-    send_x()
-    compute()
-    forward_x()
-    compute()
+    late_sibling()
+    send_x()
+    compute()
+    forward_y()
+    sib_own()
+    send_x()
+    send_late()
+    send_y()
+    forward_x()
+    sib_far()
+    sib_own()
+    send_y()
+    compute()
+    sib_own()
+    forward_y()
+    send_late()
+    sib_near()
+    send_x()
+    sib_own()
+    send_y()
+    compute()
+    sib_far()
+    late_sibling()
+    compute()
+    sib_own()
+    compute()
+    sib_own()
+    forward_x()
+    send_x()
+    sib_near()
+    late_sibling()
+    send_y()
+    send_x()
+    compute()
+    compute()
+    sib_far()
+    compute()
+    forward_x()
+    compute()
+    send_x()
     send_x()
     send_c()
-    sib_near()
-    send_x()
-    late_sibling()
-    forward_y()
-    sib_far()
-    compute()
-    compute()
-    send_y()
+    sib_far()
+    late_sibling()
+    forward_y()
+    compute()
+    compute()
     send_c()
-    forward_x()
-    sib_near()
-    late_sibling()
-    sib_far()
-    compute()
-    forward_x()
-    compute()
+    send_y()
+    forward_x()
+    send_x()
+    sib_near()
+    late_sibling()
+    sib_far()
+    compute()
+    compute()
+    forward_x()
     compute()
     send_c()
-    sib_near()
-    forward_y()
-    compute()
-    sib_far()
-    compute()
+    sib_far()
+    sib_near()
+    forward_y()
     sib_near()
     compute()
     compute()

time: 71.8 us -> 71.7 us (level)
  no operation moved by 1% of the time
where the time goes in v14:
time: 71.7 us; the launch traced here: 71.6 us
  Pallas kernels  70.7 us (99%)
  local copies, waits for them, and re-layouts  0.97 us (1%)
    pallas_call x1, Pallas kernels, product(): pl.pallas_call(kernel, out_shape=pltpu.VMEM((rows, width), jnp.bfloat16),...  70.7 us

profile of v14, /device:TPU:1, one launch (start us, length us, event | category | flops | bytes accessed | tf_op | source)
XLA Modules:
  0.0 71.6 jit_solution(11565181845746551831)
XLA Ops:
  0.0 70.7 %shard_map.28 = bf16[256,2048]{1,0:T(8,128)(2,1)S(1)} custom-call(bf16[256,2048]{1,0:T(8,128)(2,1)} %a_ref.1, bf16[256,2048]{1,0:T(8,128)(2,1)} %b_ref.1), custom_call_target="tpu_custom_call" | custom-call | tf_op jit(solution)/shard_map/pallas_call | solution.py:461
  70.7 1.0 %copy.4 = bf16[256,2048]{1,0:T(8,128)(2,1)} copy(bf16[256,2048]{1,0:T(8,128)(2,1)S(1)} %shard_map.28) | data formatting | bytes 2097152

commit v15 on v13

--- a/solution.py
+++ b/solution.py
@@ -15,19 +15,19 @@
 Y_STEPS = ((0, 0), (1, 0), (0, 1), (1, 1), (2, 1), (3, 1), (2, 0), (3, 0))
 LATE = ((0, 0), (0, 1), (3, 0), (3, 1), (1, 0), (2, 0), (1, 1), (2, 1))
 PRODUCTS = (
+    (0, 1, 4, 4, ALL),
+    (0, 0, 0, 4, ALL),
     (0, 1, 0, 4, ALL),
+    (1, 1, 4, 4, OUTER),
     (0, 0, 4, 4, ALL),
-    (0, 1, 4, 4, ALL),
     (1, 1, 0, 4, OUTER),
-    (1, 1, 4, 4, OUTER),
-    (0, 0, 0, 4, ALL),
+    (2, 1, 0, 4, ALL),
     (1, 0, 4, 4, OUTER),
-    (2, 1, 4, 4, ALL),
-    (2, 1, 0, 4, ALL),
+    (1, 0, 0, 4, OUTER),
     (1, 1, 0, 4, INNER),
     (3, 1, 0, 2, ALL),
     (1, 0, 0, 4, INNER),
-    (1, 0, 0, 4, OUTER),
+    (2, 1, 4, 4, ALL),
     (3, 1, 2, 2, ALL),
     (1, 1, 4, 4, INNER),
     (3, 1, 4, 2, ALL),
@@ -35,8 +35,8 @@
     (3, 1, 6, 1, ALL),
     (2, 0, 4, 4, ALL),
     (3, 1, 7, 1, ALL),
+    (3, 0, 0, 8, NEAR),
     (2, 0, 0, 4, ALL),
-    (3, 0, 0, 8, NEAR),
     (3, 0, 0, 8, FAR),
 )
 BIG, SMALL = range(2)
@@ -321,122 +321,122 @@
 
     b_load.wait()
     send_y()
-    send_y()
+    send_x()
     send_pair()
     send_x()
+    send_y()
+    send_y()
     send_z_early()
-    sib_own()
-    send_x()
-    send_y()
+    send_late()
     send_z_pair()
-    send_y()
-    send_x()
-    sib_own()
     send_pair()
-    send_late()
-    send_y()
-    send_late()
+    send_x()
+    send_late()
+    send_y()
     forward_x()
     send_pair()
     send_y()
-    late_sibling()
-    forward_y()
+    forward_y()
+    late_sibling()
+    forward_y()
+    late_sibling()
+    send_y()
+    send_late()
+    send_x()
+    send_late()
+    forward_x()
+    send_x()
+    send_z_mirror()
+    send_late()
+    sib_near()
+    sib_own()
+    send_full()
+    forward_y()
+    sib_far()
     send_pair()
-    send_late()
-    forward_y()
-    sib_near()
-    late_sibling()
-    forward_x()
+    sib_near()
+    late_sibling()
     send_full()
-    send_late()
-    send_x()
-    send_z_mirror()
-    forward_y()
-    send_x()
-    sib_near()
-    send_late()
+    send_x()
+    send_late()
+    send_y()
+    send_y()
     send_y()
     send_full()
-    send_x()
-    send_late()
-    late_sibling()
-    send_y()
-    send_y()
-    sib_far()
-    sib_own()
-    forward_y()
-    send_y()
-    sib_far()
-    send_y()
-    send_y()
-    forward_x()
-    compute()
-    compute()
-    send_late()
-    sib_near()
+    forward_x()
+    sib_own()
+    forward_y()
+    compute()
+    sib_far()
+    compute()
+    send_y()
+    send_x()
+    send_y()
+    send_x()
+    send_y()
+    sib_near()
+    send_late()
+    compute()
+    send_x()
+    late_sibling()
+    forward_y()
     send_full()
-    send_x()
-    send_x()
-    compute()
-    late_sibling()
-    send_x()
-    forward_y()
-    compute()
-    send_x()
-    send_full()
-    sib_own()
-    compute()
-    compute()
-    forward_x()
-    send_y()
-    send_x()
-    compute()
-    forward_y()
-    late_sibling()
-    sib_far()
-    forward_x()
-    send_y()
-    send_x()
-    send_y()
-    sib_near()
-    send_late()
-    compute()
-    sib_own()
-    send_x()
-    late_sibling()
-    sib_far()
-    sib_own()
-    compute()
-    sib_own()
-    compute()
-    forward_x()
+    sib_own()
+    send_x()
+    forward_x()
+    sib_far()
+    send_late()
+    forward_y()
+    compute()
+    send_y()
+    send_y()
+    send_x()
+    sib_own()
+    forward_x()
+    compute()
+    sib_near()
+    late_sibling()
+    sib_own()
+    late_sibling()
+    compute()
+    send_x()
+    send_x()
+    sib_near()
+    compute()
+    compute()
+    send_y()
+    sib_far()
+    compute()
+    forward_x()
+    compute()
     compute()
     send_c()
-    sib_far()
-    send_x()
-    send_x()
-    sib_near()
-    compute()
-    forward_y()
-    compute()
-    late_sibling()
-    sib_near()
-    forward_x()
+    late_sibling()
+    send_x()
+    sib_own()
+    sib_far()
+    forward_y()
+    send_x()
+    compute()
+    compute()
     compute()
     send_c()
     late_sibling()
-    send_x()
-    send_y()
+    send_y()
+    sib_near()
+    forward_x()
+    send_x()
     sib_far()
     sib_near()
     compute()
     forward_x()
     compute()
     send_c()
-    sib_far()
-    forward_y()
-    sib_own()
-    compute()
+    forward_y()
+    sib_own()
+    sib_far()
+    compute()
+    sib_own()
     sib_near()
     compute()
     send_c()

time: 71.6 us -> 71.5 us (level)
  no operation moved by 1% of the time
where the time goes in v15:
time: 71.5 us; the launch traced here: 71.4 us
  Pallas kernels  70.4 us (98%)
  local copies, waits for them, and re-layouts  0.97 us (1%)
    pallas_call x1, Pallas kernels, product(): pl.pallas_call(kernel, out_shape=pltpu.VMEM((rows, width), jnp.bfloat16),...  70.4 us

profile of v15, /device:TPU:1, one launch (start us, length us, event | category | flops | bytes accessed | tf_op | source)
XLA Modules:
  0.0 71.4 jit_solution(6602067361392331088)
XLA Ops:
  0.0 70.4 %shard_map.28 = bf16[256,2048]{1,0:T(8,128)(2,1)S(1)} custom-call(bf16[256,2048]{1,0:T(8,128)(2,1)} %a_ref.1, bf16[256,2048]{1,0:T(8,128)(2,1)} %b_ref.1), custom_call_target="tpu_custom_call" | custom-call | tf_op jit(solution)/shard_map/pallas_call | solution.py:461
  70.5 1.0 %copy.4 = bf16[256,2048]{1,0:T(8,128)(2,1)} copy(bf16[256,2048]{1,0:T(8,128)(2,1)S(1)} %shard_map.28) | data formatting | bytes 2097152

commit v16 on v11

--- a/solution.py
+++ b/solution.py
@@ -15,28 +15,28 @@
 Y_STEPS = ((0, 0), (1, 0), (0, 1), (1, 1), (2, 1), (3, 1), (2, 0), (3, 0))
 LATE = ((0, 0), (0, 1), (3, 0), (3, 1), (1, 0), (2, 0), (1, 1), (2, 1))
 PRODUCTS = (
-    (0, 1, 4, 4, ALL),
     (0, 0, 0, 4, ALL),
     (0, 1, 0, 4, ALL),
+    (0, 0, 4, 4, ALL),
+    (1, 0, 4, 4, OUTER),
+    (0, 1, 4, 4, ALL),
     (1, 0, 0, 4, OUTER),
     (1, 1, 0, 4, OUTER),
-    (1, 1, 4, 4, OUTER),
+    (2, 1, 0, 4, ALL),
     (1, 1, 0, 4, INNER),
-    (2, 1, 0, 4, ALL),
+    (1, 0, 0, 4, INNER),
     (3, 1, 0, 2, ALL),
     (2, 1, 4, 4, ALL),
+    (1, 1, 4, 4, OUTER),
     (3, 1, 2, 2, ALL),
-    (1, 0, 0, 4, INNER),
     (1, 1, 4, 4, INNER),
     (3, 1, 4, 2, ALL),
-    (0, 0, 4, 4, ALL),
     (1, 0, 4, 4, INNER),
-    (1, 0, 4, 4, OUTER),
     (3, 1, 6, 1, ALL),
     (2, 0, 4, 4, ALL),
     (3, 1, 7, 1, ALL),
+    (2, 0, 0, 4, ALL),
     (3, 0, 0, 8, NEAR),
-    (2, 0, 0, 4, ALL),
     (3, 0, 0, 8, FAR),
 )
 BIG, SMALL = range(2)
@@ -320,127 +320,127 @@
         remote(stage.at[:, pl.ds(first * unit, count * unit)], out_ref.at[:, at], BIG, c_recv, to_pair).start()
 
     b_load.wait()
-    send_x()
-    send_y()
+    send_y()
+    send_x()
     send_pair()
-    send_late()
     send_z_pair()
-    send_x()
+    send_y()
+    send_y()
     send_pair()
+    send_x()
+    send_pair()
+    send_late()
     send_z_early()
-    send_late()
-    send_y()
-    send_y()
-    send_y()
+    send_y()
+    send_late()
+    late_sibling()
+    send_y()
+    send_x()
+    forward_x()
+    forward_y()
+    send_late()
+    sib_own()
+    send_late()
+    send_full()
+    send_y()
+    forward_x()
+    sib_own()
     send_pair()
     forward_y()
-    send_y()
-    send_y()
-    forward_x()
-    forward_y()
-    send_late()
-    send_x()
-    sib_own()
-    late_sibling()
-    send_pair()
-    send_x()
-    send_late()
-    sib_far()
-    send_x()
+    send_x()
+    send_x()
+    sib_near()
+    send_z_mirror()
+    late_sibling()
+    forward_y()
+    send_y()
+    sib_far()
     send_full()
-    forward_y()
-    late_sibling()
-    send_z_mirror()
-    sib_near()
-    forward_x()
+    send_x()
+    compute()
+    send_y()
     send_full()
-    send_x()
-    late_sibling()
-    send_y()
-    send_y()
+    send_late()
+    forward_x()
+    send_y()
+    send_y()
+    compute()
+    send_late()
+    late_sibling()
+    forward_y()
+    send_x()
+    send_late()
+    send_y()
+    sib_own()
+    forward_y()
+    send_late()
+    sib_near()
+    send_y()
+    sib_own()
+    compute()
+    send_x()
+    send_x()
+    sib_far()
+    late_sibling()
+    send_x()
+    compute()
     send_full()
-    sib_near()
-    send_late()
-    forward_y()
-    compute()
-    sib_own()
-    sib_far()
-    forward_x()
-    send_y()
-    send_y()
-    sib_own()
-    send_late()
-    send_y()
-    send_late()
-    sib_near()
-    sib_own()
-    send_x()
-    send_full()
-    send_x()
-    compute()
-    send_x()
-    send_x()
-    late_sibling()
-    send_y()
-    forward_y()
-    sib_own()
-    send_y()
-    sib_own()
-    compute()
-    forward_y()
-    forward_x()
-    sib_own()
-    sib_far()
-    late_sibling()
-    send_y()
-    send_x()
-    compute()
-    send_late()
-    compute()
-    late_sibling()
-    send_y()
-    forward_x()
-    send_x()
-    send_x()
-    compute()
-    sib_own()
-    sib_near()
-    compute()
-    sib_far()
-    send_x()
-    compute()
-    forward_x()
-    compute()
-    send_x()
+    send_y()
+    compute()
+    late_sibling()
+    compute()
+    forward_x()
+    sib_near()
+    forward_y()
+    send_x()
+    send_y()
+    sib_far()
+    forward_x()
+    send_x()
+    send_y()
+    compute()
+    late_sibling()
+    send_x()
+    compute()
+    sib_near()
+    sib_own()
+    sib_far()
+    sib_own()
+    sib_near()
+    compute()
+    compute()
+    forward_x()
+    compute()
     send_c()
-    sib_near()
-    send_x()
-    late_sibling()
-    forward_y()
-    sib_far()
-    compute()
-    compute()
-    send_y()
+    sib_far()
+    sib_own()
+    forward_y()
+    send_x()
+    send_x()
+    compute()
+    sib_own()
+    late_sibling()
+    compute()
+    send_y()
+    compute()
+    sib_near()
     send_c()
     forward_x()
-    sib_near()
-    late_sibling()
-    sib_far()
-    compute()
-    forward_x()
-    compute()
+    send_x()
+    late_sibling()
+    sib_far()
+    sib_near()
+    compute()
+    forward_x()
     compute()
     send_c()
-    sib_near()
-    forward_y()
-    compute()
-    sib_far()
-    compute()
-    sib_near()
-    compute()
-    compute()
-    sib_far()
+    forward_y()
+    sib_far()
+    sib_near()
+    compute()
+    compute()
     send_c()
+    sib_far()
     compute()
     compute()
     send_c()

time: 71.8 us -> 71.8 us (level)
  no operation moved by 1% of the time
where the time goes in v16:
time: 71.8 us
  Pallas kernels  70.8 us (99%)
  local copies, waits for them, and re-layouts  0.97 us (1%)
    pallas_call x1, Pallas kernels, product(): pl.pallas_call(kernel, out_shape=pltpu.VMEM((rows, width), jnp.bfloat16),...  70.8 us

profile of v16, /device:TPU:1, one launch (start us, length us, event | category | flops | bytes accessed | tf_op | source)
XLA Modules:
  0.0 71.8 jit_solution(18169983190610249733)
XLA Ops:
  0.0 70.8 %shard_map.28 = bf16[256,2048]{1,0:T(8,128)(2,1)S(1)} custom-call(bf16[256,2048]{1,0:T(8,128)(2,1)} %a_ref.1, bf16[256,2048]{1,0:T(8,128)(2,1)} %b_ref.1), custom_call_target="tpu_custom_call" | custom-call | tf_op jit(solution)/shard_map/pallas_call | solution.py:461
  70.8 1.0 %copy.4 = bf16[256,2048]{1,0:T(8,128)(2,1)} copy(bf16[256,2048]{1,0:T(8,128)(2,1)S(1)} %shard_map.28) | data formatting | bytes 2097152

commit v17 on v13

--- a/solution.py
+++ b/solution.py
@@ -15,27 +15,27 @@
 Y_STEPS = ((0, 0), (1, 0), (0, 1), (1, 1), (2, 1), (3, 1), (2, 0), (3, 0))
 LATE = ((0, 0), (0, 1), (3, 0), (3, 1), (1, 0), (2, 0), (1, 1), (2, 1))
 PRODUCTS = (
+    (0, 1, 4, 4, ALL),
     (0, 1, 0, 4, ALL),
-    (0, 0, 4, 4, ALL),
-    (0, 1, 4, 4, ALL),
+    (0, 0, 0, 4, ALL),
     (1, 1, 0, 4, OUTER),
     (1, 1, 4, 4, OUTER),
-    (0, 0, 0, 4, ALL),
-    (1, 0, 4, 4, OUTER),
+    (0, 0, 4, 4, ALL),
     (2, 1, 4, 4, ALL),
     (2, 1, 0, 4, ALL),
     (1, 1, 0, 4, INNER),
     (3, 1, 0, 2, ALL),
-    (1, 0, 0, 4, INNER),
     (1, 0, 0, 4, OUTER),
+    (1, 0, 4, 4, OUTER),
     (3, 1, 2, 2, ALL),
     (1, 1, 4, 4, INNER),
     (3, 1, 4, 2, ALL),
+    (1, 0, 0, 4, INNER),
     (1, 0, 4, 4, INNER),
     (3, 1, 6, 1, ALL),
+    (2, 0, 0, 4, ALL),
+    (3, 1, 7, 1, ALL),
     (2, 0, 4, 4, ALL),
-    (3, 1, 7, 1, ALL),
-    (2, 0, 0, 4, ALL),
     (3, 0, 0, 8, NEAR),
     (3, 0, 0, 8, FAR),
 )
@@ -321,123 +321,123 @@
 
     b_load.wait()
     send_y()
+    send_x()
     send_y()
     send_pair()
     send_x()
+    send_z_pair()
     send_z_early()
-    sib_own()
-    send_x()
-    send_y()
-    send_z_pair()
-    send_y()
-    send_x()
-    sib_own()
+    send_y()
+    send_late()
+    forward_y()
+    late_sibling()
+    send_late()
+    forward_x()
     send_pair()
-    send_late()
-    send_y()
-    send_late()
-    forward_x()
+    send_y()
+    send_y()
+    send_y()
+    send_late()
+    send_x()
+    send_late()
+    send_x()
     send_pair()
-    send_y()
-    late_sibling()
+    send_full()
+    send_x()
+    sib_own()
     forward_y()
     send_pair()
-    send_late()
-    forward_y()
-    sib_near()
-    late_sibling()
-    forward_x()
+    send_z_mirror()
+    send_late()
+    sib_far()
+    send_x()
+    forward_y()
+    late_sibling()
+    send_y()
+    late_sibling()
+    forward_x()
+    send_y()
     send_full()
-    send_late()
-    send_x()
-    send_z_mirror()
-    forward_y()
-    send_x()
-    sib_near()
-    send_late()
-    send_y()
+    send_y()
+    forward_x()
+    sib_near()
+    send_y()
+    send_late()
     send_full()
-    send_x()
-    send_late()
-    late_sibling()
-    send_y()
-    send_y()
-    sib_far()
-    sib_own()
-    forward_y()
-    send_y()
-    sib_far()
-    send_y()
-    send_y()
-    forward_x()
-    compute()
-    compute()
-    send_late()
-    sib_near()
+    send_y()
+    send_y()
+    forward_y()
+    send_late()
+    send_x()
+    sib_own()
+    sib_own()
+    forward_y()
+    sib_near()
+    compute()
+    sib_far()
+    send_late()
     send_full()
     send_x()
-    send_x()
-    compute()
-    late_sibling()
-    send_x()
-    forward_y()
-    compute()
-    send_x()
-    send_full()
-    sib_own()
-    compute()
-    compute()
-    forward_x()
-    send_y()
-    send_x()
-    compute()
-    forward_y()
-    late_sibling()
-    sib_far()
-    forward_x()
-    send_y()
-    send_x()
-    send_y()
-    sib_near()
-    send_late()
-    compute()
-    sib_own()
-    send_x()
-    late_sibling()
-    sib_far()
-    sib_own()
-    compute()
-    sib_own()
-    compute()
-    forward_x()
-    compute()
+    late_sibling()
+    send_x()
+    forward_y()
+    compute()
+    send_x()
+    compute()
+    sib_own()
+    late_sibling()
+    sib_far()
+    send_y()
+    forward_x()
+    sib_near()
+    send_x()
+    compute()
+    forward_x()
+    send_y()
+    sib_near()
+    compute()
+    compute()
+    send_y()
+    send_x()
+    late_sibling()
+    sib_near()
+    sib_own()
+    compute()
+    sib_far()
+    send_x()
+    compute()
+    compute()
+    forward_x()
+    compute()
+    forward_y()
     send_c()
-    sib_far()
-    send_x()
-    send_x()
-    sib_near()
-    compute()
-    forward_y()
-    compute()
-    late_sibling()
-    sib_near()
-    forward_x()
+    send_x()
+    compute()
+    sib_far()
+    send_y()
+    compute()
+    send_x()
+    sib_near()
+    forward_x()
+    late_sibling()
+    sib_own()
     compute()
     send_c()
-    late_sibling()
-    send_x()
-    send_y()
-    sib_far()
-    sib_near()
-    compute()
-    forward_x()
-    compute()
+    sib_own()
+    send_x()
+    late_sibling()
+    sib_far()
+    compute()
+    forward_x()
+    forward_y()
+    compute()
+    sib_near()
     send_c()
     sib_far()
-    forward_y()
-    sib_own()
-    compute()
-    sib_near()
+    sib_own()
+    compute()
+    sib_near()
+    compute()
     compute()
     send_c()
     sib_far()

time: 71.6 us -> 71.5 us (level)
  no operation moved by 1% of the time
where the time goes in v17:
time: 71.5 us; the launch traced here: 71.4 us
  Pallas kernels  70.4 us (98%)
  local copies, waits for them, and re-layouts  0.97 us (1%)
    pallas_call x1, Pallas kernels, product(): pl.pallas_call(kernel, out_shape=pltpu.VMEM((rows, width), jnp.bfloat16),...  70.4 us

profile of v17, /device:TPU:1, one launch (start us, length us, event | category | flops | bytes accessed | tf_op | source)
XLA Modules:
  0.0 71.4 jit_solution(2036625928407970356)
XLA Ops:
  0.0 70.4 %shard_map.28 = bf16[256,2048]{1,0:T(8,128)(2,1)S(1)} custom-call(bf16[256,2048]{1,0:T(8,128)(2,1)} %a_ref.1, bf16[256,2048]{1,0:T(8,128)(2,1)} %b_ref.1), custom_call_target="tpu_custom_call" | custom-call | tf_op jit(solution)/shard_map/pallas_call | solution.py:461
  70.4 1.0 %copy.4 = bf16[256,2048]{1,0:T(8,128)(2,1)} copy(bf16[256,2048]{1,0:T(8,128)(2,1)S(1)} %shard_map.28) | data formatting | bytes 2097152

commit v18 on v14

--- a/solution.py
+++ b/solution.py
@@ -15,28 +15,28 @@
 Y_STEPS = ((0, 0), (1, 0), (0, 1), (1, 1), (2, 1), (3, 1), (2, 0), (3, 0))
 LATE = ((0, 0), (0, 1), (3, 0), (3, 1), (1, 0), (2, 0), (1, 1), (2, 1))
 PRODUCTS = (
-    (0, 0, 4, 4, ALL),
     (0, 1, 4, 4, ALL),
     (0, 0, 0, 4, ALL),
-    (1, 1, 4, 4, OUTER),
+    (0, 0, 4, 4, ALL),
+    (0, 1, 0, 4, ALL),
     (1, 0, 0, 4, OUTER),
     (1, 0, 4, 4, OUTER),
-    (0, 1, 0, 4, ALL),
     (1, 1, 0, 4, OUTER),
     (2, 1, 0, 4, ALL),
+    (1, 1, 4, 4, OUTER),
     (1, 1, 0, 4, INNER),
     (3, 1, 0, 2, ALL),
+    (1, 0, 0, 4, INNER),
     (2, 1, 4, 4, ALL),
     (3, 1, 2, 2, ALL),
-    (1, 0, 0, 4, INNER),
     (1, 1, 4, 4, INNER),
     (3, 1, 4, 2, ALL),
     (1, 0, 4, 4, INNER),
     (3, 1, 6, 1, ALL),
+    (2, 0, 4, 4, ALL),
+    (3, 1, 7, 1, ALL),
+    (3, 0, 0, 8, NEAR),
     (2, 0, 0, 4, ALL),
-    (3, 1, 7, 1, ALL),
-    (2, 0, 4, 4, ALL),
-    (3, 0, 0, 8, NEAR),
     (3, 0, 0, 8, FAR),
 )
 BIG, SMALL = range(2)
@@ -322,125 +322,125 @@
     b_load.wait()
     send_y()
     send_x()
-    send_x()
-    send_y()
+    sib_own()
+    send_y()
+    send_late()
+    send_pair()
+    send_x()
+    send_y()
+    send_z_pair()
     send_y()
     send_z_early()
+    send_x()
+    forward_y()
+    send_x()
+    send_y()
+    send_late()
+    forward_x()
+    send_late()
+    forward_x()
+    sib_own()
     send_pair()
-    send_z_pair()
-    sib_own()
-    send_late()
-    send_y()
+    forward_y()
+    late_sibling()
+    send_late()
     send_y()
     send_pair()
-    send_y()
-    send_x()
-    send_late()
+    forward_y()
+    send_x()
     send_pair()
-    sib_own()
-    forward_x()
-    forward_y()
-    send_late()
-    send_late()
-    forward_x()
-    forward_y()
-    forward_y()
-    send_pair()
-    send_x()
     send_z_mirror()
-    send_x()
-    late_sibling()
-    send_y()
-    send_y()
-    sib_far()
-    sib_near()
-    late_sibling()
+    send_y()
     send_full()
-    send_x()
-    send_y()
-    forward_x()
+    send_y()
     send_full()
-    forward_y()
-    sib_near()
-    send_late()
-    compute()
-    send_y()
-    send_x()
-    send_late()
-    send_y()
-    late_sibling()
-    send_x()
-    compute()
-    sib_near()
+    sib_near()
+    send_x()
+    send_y()
+    forward_x()
+    send_y()
+    late_sibling()
+    sib_far()
+    late_sibling()
+    send_late()
+    compute()
+    compute()
     send_full()
+    send_late()
+    sib_far()
+    forward_y()
+    send_y()
+    send_x()
     send_full()
-    late_sibling()
-    send_x()
-    compute()
-    forward_y()
-    sib_own()
-    send_x()
-    send_late()
-    send_y()
-    forward_x()
-    sib_far()
-    sib_own()
-    send_y()
-    compute()
-    sib_own()
-    forward_y()
-    send_late()
-    sib_near()
-    send_x()
-    sib_own()
-    send_y()
-    compute()
-    sib_far()
-    late_sibling()
-    compute()
-    sib_own()
-    compute()
-    sib_own()
-    forward_x()
-    send_x()
-    sib_near()
-    late_sibling()
-    send_y()
-    send_x()
-    compute()
-    compute()
-    sib_far()
-    compute()
-    forward_x()
-    compute()
-    send_x()
+    sib_near()
+    forward_y()
+    compute()
+    send_x()
+    compute()
+    send_late()
+    sib_own()
+    send_x()
+    sib_near()
+    send_y()
+    sib_own()
+    send_x()
+    compute()
+    forward_x()
+    sib_own()
+    send_x()
+    forward_y()
+    send_y()
+    sib_far()
+    late_sibling()
+    send_y()
+    sib_own()
+    send_late()
+    compute()
+    forward_x()
+    compute()
+    send_x()
+    sib_near()
+    sib_own()
+    late_sibling()
+    send_y()
+    compute()
+    late_sibling()
+    compute()
+    sib_far()
+    send_x()
+    forward_x()
+    compute()
+    compute()
     send_x()
     send_c()
-    sib_far()
-    late_sibling()
-    forward_y()
-    compute()
-    compute()
+    sib_near()
+    sib_far()
+    send_x()
+    compute()
+    forward_y()
+    compute()
+    compute()
+    send_y()
+    late_sibling()
+    forward_x()
+    send_x()
     send_c()
-    send_y()
-    forward_x()
-    send_x()
-    sib_near()
-    late_sibling()
-    sib_far()
-    compute()
+    sib_own()
+    late_sibling()
+    sib_near()
+    sib_far()
+    sib_near()
     compute()
     forward_x()
     compute()
     send_c()
     sib_far()
-    sib_near()
-    forward_y()
-    sib_near()
-    compute()
-    compute()
-    sib_far()
+    forward_y()
+    sib_near()
+    compute()
+    compute()
     send_c()
+    sib_far()
     compute()
     compute()
     send_c()

time: 71.7 us -> 71.2 us (level)
  no operation moved by 1% of the time
where the time goes in v18:
time: 71.2 us; the launch traced here: 71.1 us
  Pallas kernels  70.1 us (98%)
  local copies, waits for them, and re-layouts  0.97 us (1%)
    pallas_call x1, Pallas kernels, product(): pl.pallas_call(kernel, out_shape=pltpu.VMEM((rows, width), jnp.bfloat16),...  70.1 us

profile of v18, /device:TPU:1, one launch (start us, length us, event | category | flops | bytes accessed | tf_op | source)
XLA Modules:
  0.0 71.1 jit_solution(3797650185863913401)
XLA Ops:
  0.0 70.1 %shard_map.28 = bf16[256,2048]{1,0:T(8,128)(2,1)S(1)} custom-call(bf16[256,2048]{1,0:T(8,128)(2,1)} %a_ref.1, bf16[256,2048]{1,0:T(8,128)(2,1)} %b_ref.1), custom_call_target="tpu_custom_call" | custom-call | tf_op jit(solution)/shard_map/pallas_call | solution.py:461
  70.1 1.0 %copy.4 = bf16[256,2048]{1,0:T(8,128)(2,1)} copy(bf16[256,2048]{1,0:T(8,128)(2,1)S(1)} %shard_map.28) | data formatting | bytes 2097152
